TPU v7x, 32 devices: a whole 2x2x4 slice. The times are simulated.
32 devices in a mesh: gx: 4 (over z), gy: 4 (over y, core), gz: 2 (over x).
Axes of the slice: x: 2, y: 2, z: 4, core: 2. Of those that a mesh axis runs over, the one named last changes fastest.
Arguments:
- coarse_source: float32 [64, 128, 256], P('gx', 'gy', 'gz'), may hold values from -6 to 6
- coarse_shift: float32 [64, 128, 256], P('gx', 'gy', 'gz'), may hold values from 0.1 to 4
- coarse_start: float32 [64, 128, 256], P('gx', 'gy', 'gz'), may hold values from -3 to 3
- fine_source: float32 [128, 32768], P(('gx', 'gy', 'gz')), may hold values from -6 to 6
- fine_shift: float32 [128, 32768], P(('gx', 'gy', 'gz')), may hold values from 0.1 to 4
- fine_start: float32 [128, 32768], P(('gx', 'gy', 'gz')), may hold values from -3 to 3
- box_corner: int32 [32, 4, 3], P(('gx', 'gy', 'gz')), may hold values from 0 to 480, as said below
- box_owner: int32 [32, 4], P(('gx', 'gy', 'gz')), may hold values from 0 to 8, as said below
Outputs:
- potential: float32 [64, 128, 256], P('gx', 'gy', 'gz')
- fine_solution: float32 [128, 32768], P(('gx', 'gy', 'gz'))
- residual_norms: float32 [2], replicated
Inputs may be any that keep to these rules, and one draw needn't show every extreme that they name: `box_owner`: each device has at least one live slot; in every group of 8 devices that share a gx index some device has 4 live slots; the live owners of one device are distinct; no device is the owner of more than 4 live boxes, and in every group some device is the owner of exactly 4 live boxes. `box_corner`: each corner is a multiple of 32 and its footprint lies in the coarse block of the device that lists it; the 4 footprints of one device are distinct.
All inputs are finite; a program needn't handle non-finite values.
Results may differ from a plain program's by a relative error of at most 0.0001.
Values sent between devices are 32-bit elements; how exact they have to be, the bound alone decides.
A program may use at most 128 MiB of HBM per device.

v0:
```python
import functools

import jax
import jax.numpy as jnp
from jax import lax
from jax.experimental import pallas as pl
from jax.experimental.pallas import tpu as pltpu
from jax.sharding import PartitionSpec as P

FOOT = 16
CYCLES = 2
CSWEEPS = 4
FSWEEPS = 3
OMEGA = 0.8
KEEP = 1.0 - OMEGA
MESH = pl.DeviceIdType.MESH
LANES = 128
SIDE = 2 * FOOT


def take(x, idx):
    return jnp.take_along_axis(x, idx, axis=1, mode="promise_in_bounds")


def iota(shape, dim):
    return lax.broadcasted_iota(jnp.int32, shape, dim)


def kernel(
    sizes,
    corner,
    owner,
    c_src_hbm,
    c_shift_hbm,
    c_start_hbm,
    f_src_hbm,
    f_shift_hbm,
    f_start_hbm,
    pot_out,
    fine_out,
    norm_out,
    c_src,
    c_shift,
    f_src,
    f_shift,
    f_start,
    in_sem,
    U,
    W,
    comp,
    yh,
    ys,
    zh,
    zs,
    V,
    FW,
    FS,
    FD,
    G,
    compact,
    R,
    pout,
    prec,
    rout,
    rrec,
    slotid,
    sums,
    xsum,
    p_send,
    p_recv,
    r_send,
    r_recv,
    h_send,
    h_recv,
    n_send,
    n_recv,
):
    n_gx, n_gy, n_gz = sizes
    group = n_gy * n_gz
    slots = owner.shape[1]
    nx, ny, nz = c_src_hbm.shape
    along_y = ny // FOOT
    gx, gy, gz = lax.axis_index("gx"), lax.axis_index("gy"), lax.axis_index("gz")
    me = gy * n_gz + gz

    def rank_id(rank):
        return (gx, rank // n_gz, rank % n_gz)

    have = (gx > 0, gx < n_gx - 1, gy > 0, gy < n_gy - 1, gz > 0, gz < n_gz - 1)
    beside = (
        (gx - 1, gy, gz),
        (gx + 1, gy, gz),
        (gx, gy - 1, gz),
        (gx, gy + 1, gz),
        (gx, gy, gz - 1),
        (gx, gy, gz + 1),
    )

    loads = [
        pltpu.make_async_copy(source, target, in_sem.at[i])
        for i, (source, target) in enumerate(
            (
                (c_start_hbm, U.at[0, pl.ds(1, nx)]),
                (c_shift_hbm, c_shift),
                (f_start_hbm, f_start),
                (f_src_hbm, f_src),
                (f_shift_hbm, f_shift),
                (c_src_hbm, c_src),
            )
        )
    ]
    for load in loads:
        load.start()

    for p in range(2):
        U[p, 0] = jnp.zeros((ny, nz), jnp.float32)
        U[p, nx + 1] = jnp.zeros((ny, nz), jnp.float32)
    yh[...] = jnp.zeros_like(yh)
    zh[...] = jnp.zeros_like(zh)

    barrier = pltpu.get_barrier_semaphore()
    for d in range(1, group):
        pl.semaphore_signal(barrier, inc=1, device_id=rank_id((me + d) % group), device_id_type=MESH)
    for d in range(1, n_gx):
        pl.semaphore_signal(barrier, inc=1, device_id=((gx + d) % n_gx, gy, gz), device_id_type=MESH)
    pl.semaphore_wait(barrier, group - 1 + n_gx - 1)

    tile = (8, LANES)
    lane = iota(tile, 1)
    sub = iota(tile, 0)
    wide = (ny, LANES)
    wlane = iota(wide, 1)
    wsub = iota(wide, 0)
    box_row = []
    box_col = []
    box_live = []
    for s in range(slots):
        box_row.append((corner[1, 0, s] // 2 - gy * ny) // FOOT)
        box_col.append((corner[2, 0, s] // 2 - gz * nz) // FOOT)
        box_live.append(owner[0, s] < group)

    def exchange(out, rec, send, recv, rows):
        copies = []
        for d in range(1, group):
            peer = (me + d) % group
            copy = pltpu.make_async_remote_copy(
                src_ref=out.at[peer, pl.ds(0, rows)],
                dst_ref=rec.at[me, pl.ds(0, rows)],
                send_sem=send.at[d],
                recv_sem=recv.at[d],
                device_id=rank_id(peer),
                device_id_type=MESH,
            )
            copy.start()
            copies.append(copy)
        rec[me, pl.ds(0, rows)] = out[me, pl.ds(0, rows)]
        return copies

    def arrive(out, rec, send, recv, rows):
        for d in range(1, group):
            source = (me + group - d) % group
            pltpu.make_async_remote_copy(
                src_ref=out.at[source, pl.ds(0, rows)],
                dst_ref=rec.at[source, pl.ds(0, rows)],
                send_sem=send.at[d],
                recv_sem=recv.at[d],
                device_id=rank_id(source),
                device_id_type=MESH,
            ).wait_recv()

    def pack_parents(p):
        @pl.loop(0, FOOT // 4)
        def _(xg):
            for s in range(slots):
                idx = box_col[s] * FOOT + (lane % FOOT)
                acc = jnp.zeros(tile, jnp.float32)
                for k in range(4):
                    for yl in range(2):
                        a = U[p, 1 + xg * 4 + k, pl.ds(yl, 8, stride=2), :]
                        for b in range(1, along_y):
                            other = U[p, 1 + xg * 4 + k, pl.ds(b * FOOT + yl, 8, stride=2), :]
                            a = jnp.where(box_row[s] == b, other, a)
                        acc = jnp.where(lane // FOOT == 2 * k + yl, take(a, idx), acc)
                compact[s, pl.ds(pl.multiple_of(xg * 8, 8), 8), :] = acc

        for q in range(group):
            acc = jnp.zeros((32, LANES), jnp.float32)
            flag = jnp.zeros(tile, jnp.float32)
            for s in range(slots):
                acc = jnp.where(owner[0, s] == q, compact[s], acc)
                flag = jnp.where(owner[0, s] == q, 1.0, flag)
            pout[q, pl.ds(0, 32)] = acc
            pout[q, pl.ds(32, 8)] = flag

    def slot_masks():
        count = jnp.zeros(tile, jnp.float32)
        for q in range(group):
            flag = prec[q, pl.ds(32, 8)]
            slotid[q] = jnp.where(flag > 0.5, count, -1.0)
            count = count + flag
        return count

    spread_lane = (lane // 64) * FOOT + (lane % SIDE) // 2

    def ghosts(par):
        @pl.loop(0, FOOT // 4)
        def _(xg):
            rows = pl.ds(pl.multiple_of(xg * 8, 8), 8)
            for j in range(slots):
                acc = jnp.zeros(tile, jnp.float32)
                for q in range(group):
                    acc = jnp.where(slotid[q] == float(j), prec[q, rows], acc)
                for k in range(4):
                    G[par, j, xg * 4 + k] = take(acc, k * SIDE + spread_lane)

    y_top = (lane >= 96) & (sub == 7)
    y_low = (lane < 32) & (sub == 0)
    z_pos = lane % SIDE

    def plane(x, shift=0):
        start = pl.multiple_of((x + 1) * 8, 8)
        return pl.ds(start + shift, 8)

    def beside_fine(vp, par, j, x, ghost):
        v = V[vp, j, plane(x)]
        up = jnp.where(lane < 32, V[vp, j, plane(x, 1)], v)
        up = jnp.where(y_top, ghost, pltpu.roll(up, LANES - 32, 1))
        lo = jnp.where(lane >= 96, V[vp, j, plane(x, -1)], v)
        lo = jnp.where(y_low, ghost, pltpu.roll(lo, 32, 1))
        zu = jnp.where(z_pos < SIDE - 1, pltpu.roll(v, LANES - 1, 1), ghost)
        zl = jnp.where(z_pos > 0, pltpu.roll(v, 1, 1), ghost)
        return v, ((V[vp, j, plane(x + 1)] + V[vp, j, plane(x - 1)]) + (up + lo)) + (zu + zl)

    def fine_rows(j, x):
        return pl.ds(x * 8 * slots + j, 8, stride=slots)

    def edges(vp, par):
        for j in range(slots):
            V[vp, j, plane(-1)] = G[par, j, 0]
            V[vp, j, plane(SIDE)] = G[par, j, FOOT - 1]

    def fine_sweep(vp, par):
        @pl.loop(0, FOOT, unroll=4)
        def _(X):
            for j in range(slots):
                ghost = G[par, j, X]
                for e in range(2):
                    x = 2 * X + e
                    v, s = beside_fine(vp, par, j, x, ghost)
                    V[1 - vp, j, plane(x)] = KEEP * v + FW[j, x] * (FS[j, x] + s)

    shrink_lane = ((lane % 32) // FOOT) * 64 + 2 * (lane % FOOT)

    def fine_remainder(vp, par, occupied):
        def body(X, totals):
            totals = list(totals)
            for j in range(slots):
                ghost = G[par, j, X]
                for e in range(2):
                    x = 2 * X + e
                    v, s = beside_fine(vp, par, j, x, ghost)
                    r = (FS[j, x] - FD[j, x] * v) + s
                    totals[j] = totals[j] + r * r
                    V[1 - vp, j, plane(x)] = r
            return tuple(totals)

        zero = jnp.zeros(tile, jnp.float32)
        totals = lax.fori_loop(0, FOOT, body, (zero,) * slots, unroll=4)

        @pl.loop(0, FOOT // 4)
        def _(xg):
            for j in range(slots):
                acc = zero
                for k in range(4):
                    x = 2 * (xg * 4 + k)
                    t = V[1 - vp, j, plane(x)] + V[1 - vp, j, plane(x + 1)]
                    t = t + pltpu.roll(t, LANES - 1, 1)
                    t = t + pltpu.roll(t, LANES - 32, 1)
                    acc = jnp.where(lane // 32 == k, take(t, shrink_lane), acc)
                R[j, pl.ds(pl.multiple_of(xg * 8, 8), 8)] = acc * 0.125

        total = zero
        for j in range(slots):
            total = total + jnp.where(occupied[j], totals[j], 0.0)
        return total

    def pack_returns():
        for q in range(group):
            which = slotid[q]
            for g in range(4):
                rows = pl.ds(g * 8, 8)
                acc = jnp.zeros(tile, jnp.float32)
                for j in range(slots):
                    acc = jnp.where(which == float(j), R[j, rows], acc)
                rout[q, rows] = acc

    def deposit():
        @pl.loop(0, FOOT // 4)
        def _(xg):
            rows = pl.ds(pl.multiple_of(xg * 8, 8), 8)
            tiles = []
            for s in range(slots):
                tiles.append(rrec[jnp.minimum(owner[0, s], group - 1), rows])
            for k in range(4):
                x = xg * 4 + k
                for yl in range(2):
                    idx = k * 32 + yl * FOOT + lane % FOOT
                    got = []
                    for s in range(slots):
                        col = jnp.where(box_live[s], box_col[s], -1)
                        got.append(jnp.where(lane // FOOT == col, take(tiles[s], idx), 0.0))
                    for b in range(along_y):
                        place = pl.ds(b * FOOT + yl, 8, stride=2)
                        acc = c_src[x, place, :]
                        for s in range(slots):
                            acc = acc + jnp.where(box_row[s] == b, got[s], 0.0)
                        comp[x, place, :] = acc

    def halo_copies(p, which=range(6)):
        faces = (
            (U.at[p, 1], U.at[p, nx + 1]),
            (U.at[p, nx], U.at[p, 0]),
            (ys.at[0], yh.at[p, 1]),
            (ys.at[1], yh.at[p, 0]),
            (zs.at[0], zh.at[p, 1]),
            (zs.at[1], zh.at[p, 0]),
        )
        copies = []
        for i in which:
            source, target = faces[i]
            copies.append(
                pltpu.make_async_remote_copy(
                    src_ref=source,
                    dst_ref=target,
                    send_sem=h_send.at[p, i],
                    recv_sem=h_recv.at[p, i ^ 1],
                    device_id=beside[i],
                    device_id_type=MESH,
                )
            )
        return copies

    def halo_waits(p):
        places = (
            U.at[p, 0],
            U.at[p, nx + 1],
            yh.at[p, 0],
            yh.at[p, 1],
            zh.at[p, 0],
            zh.at[p, 1],
        )
        copies = []
        for i, target in enumerate(places):
            copies.append(
                pltpu.make_async_remote_copy(
                    src_ref=target,
                    dst_ref=target,
                    send_sem=h_send.at[p, i],
                    recv_sem=h_recv.at[p, i],
                    device_id=beside[i],
                    device_id_type=MESH,
                )
            )
        return copies

    def send_halos(p, which):
        for i, copy in zip(which, halo_copies(p, which)):
            pl.when(have[i])(copy.start)

    def wait_halos(p):
        for i, (sent, got) in enumerate(zip(halo_copies(p), halo_waits(p))):

            @pl.when(have[i])
            def _():
                sent.wait_send()
                got.wait_recv()

    groups = ny // 8
    per = min(groups, LANES // nx)

    def keep_y(p):
        for x in range(nx):
            ys[0, pl.ds(x, 1), :] = U[p, x + 1, pl.ds(0, 1), :]
            ys[1, pl.ds(x, 1), :] = U[p, x + 1, pl.ds(ny - 1, 1), :]

    def keep_z(p):
        for t in range(groups // per):

            def body(x, faces):
                zlo, zhi = faces
                for g in range(per):
                    at = g * nx + x
                    u = U[p, x + 1, pl.ds((t * per + g) * 8, 8)]
                    zlo = jnp.where(lane == at, pltpu.roll(u, at, 1), zlo)
                    zhi = jnp.where(lane == at, pltpu.roll(u, (at + 1) % LANES, 1), zhi)
                return zlo, zhi

            empty = jnp.zeros(tile, jnp.float32)
            zlo, zhi = lax.fori_loop(0, nx // 4, lambda i, f: body(4 * i + 3, body(4 * i + 2, body(4 * i + 1, body(4 * i, f)))), (empty, empty))
            zs[0, pl.ds(t * 8, 8)] = zlo
            zs[1, pl.ds(t * 8, 8)] = zhi

    def send_faces(p):
        send_halos(p, (0, 1))
        keep_y(p)
        send_halos(p, (2, 3))
        keep_z(p)
        send_halos(p, (4, 5))

    def z_column(packed, x, to):
        tiles = []
        for g in range(groups):
            at = (g % per) * nx + x
            face = packed[8 * (g // per) : 8 * (g // per) + 8]
            shift = (to - at) % LANES
            tiles.append(pltpu.roll(face, shift, 1) if shift else face)
        return jnp.concatenate(tiles, axis=0)

    none = jnp.zeros(wide, jnp.float32)

    def coarse_sweep(p, want_square):
        zl = zh[p, 0]
        zu = zh[p, 1]

        total = none
        for x in range(nx):
            u = U[p, x + 1]
            ym = jnp.where(wsub == 0, yh[p, 0, pl.ds(x, 1), :], pltpu.roll(u, 1, 0))
            yp = jnp.where(wsub == ny - 1, yh[p, 1, pl.ds(x, 1), :], pltpu.roll(u, ny - 1, 0))
            zm = jnp.where(wlane == 0, z_column(zl, x, 0), pltpu.roll(u, 1, 1))
            zp = jnp.where(wlane == nz - 1, z_column(zu, x, nz - 1), pltpu.roll(u, nz - 1, 1))
            s = ((U[p, x] + U[p, x + 2]) + (ym + yp)) + (zm + zp)
            s = s + comp[x]
            U[1 - p, x + 1] = KEEP * u + W[x] * s
            if want_square:
                last = s - (6.0 + c_shift[x]) * u
                total = total + last * last
        return total

    loads[0].wait()
    pack_parents(0)
    parent_copies = exchange(pout, prec, p_send, p_recv, 40)
    send_faces(0)

    for load in loads[1:]:
        load.wait()

    @pl.loop(0, nx)
    def _(x):
        W[x] = OMEGA / (6.0 + c_shift[x])

    @pl.loop(0, SIDE)
    def _(x):
        for j in range(slots):
            rows = fine_rows(j, x)
            V[0, j, plane(x)] = f_start[rows, :]
            FS[j, x] = f_src[rows, :]
            FD[j, x] = 6.0 + f_shift[rows, :]
            FW[j, x] = OMEGA / FD[j, x]

    vp = 0
    return_copies = []
    for cycle in range(CYCLES):
        par = cycle % 2
        arrive(pout, prec, p_send, p_recv, 40)
        if cycle == 0:
            count = slot_masks()
            occupied = [count > float(j) for j in range(slots)]
        ghosts(par)
        if cycle > 0:

            @pl.loop(0, FOOT)
            def _(X):
                for j in range(slots):
                    delta = G[par, j, X] - G[1 - par, j, X]
                    for e in range(2):
                        V[vp, j, plane(2 * X + e)] = V[vp, j, plane(2 * X + e)] + delta

        edges(0, par)
        edges(1, par)
        for sweep in range(FSWEEPS):
            fine_sweep(vp, par)
            vp = 1 - vp
        square = fine_remainder(vp, par, occupied)
        for copy in return_copies:
            copy.wait_send()
        pack_returns()
        return_copies = exchange(rout, rrec, r_send, r_recv, 32)
        arrive(rout, rrec, r_send, r_recv, 32)
        deposit()
        for sweep in range(CSWEEPS):
            p = sweep % 2
            final = cycle == CYCLES - 1 and sweep == CSWEEPS - 1
            wait_halos(p)
            total = coarse_sweep(p, sweep == CSWEEPS - 1)
            if not final and sweep < CSWEEPS - 1:
                send_faces(1 - p)
        for g in range(ny // 8):
            square = square + total[8 * g : 8 * g + 8]
        sums[cycle] = square
        for copy in parent_copies:
            copy.wait_send()
        pack_parents(0)
        if cycle == CYCLES - 1:
            both = jnp.where(
                sub == 0,
                jnp.sum(sums[0], axis=0, keepdims=True),
                jnp.where(sub == 1, jnp.sum(sums[1], axis=0, keepdims=True), 0.0),
            )
            for q in range(group):
                pout[q, pl.ds(32, 8)] = both
        parent_copies = exchange(pout, prec, p_send, p_recv, 40)
        if cycle < CYCLES - 1:
            send_faces(0)

    store = pltpu.make_async_copy(U.at[0, pl.ds(1, nx)], pot_out, in_sem.at[0])
    store.start()

    for copy in return_copies:
        copy.wait_send()
    arrive(pout, prec, p_send, p_recv, 40)
    for copy in parent_copies:
        copy.wait_send()

    mine = jnp.zeros(tile, jnp.float32)
    for q in range(group):
        mine = mine + prec[q, pl.ds(32, 8)]
    xsum[gx] = mine
    norm_copies = []
    for d in range(1, n_gx):
        copy = pltpu.make_async_remote_copy(
            src_ref=xsum.at[gx],
            dst_ref=xsum.at[gx],
            send_sem=n_send.at[d],
            recv_sem=n_recv.at[d],
            device_id=((gx + d) % n_gx, gy, gz),
            device_id_type=MESH,
        )
        copy.start()
        norm_copies.append(copy)

    par = CYCLES % 2
    ghosts(par)

    @pl.loop(0, FOOT)
    def _(X):
        for j in range(slots):
            delta = G[par, j, X] - G[1 - par, j, X]
            for e in range(2):
                x = 2 * X + e
                fine_out[fine_rows(j, x), :] = jnp.where(occupied[j], V[vp, j, plane(x)] + delta, 0.0)

    for d in range(1, n_gx):
        source = (gx + n_gx - d) % n_gx
        pltpu.make_async_remote_copy(
            src_ref=xsum.at[source],
            dst_ref=xsum.at[source],
            send_sem=n_send.at[d],
            recv_sem=n_recv.at[d],
            device_id=(source, gy, gz),
            device_id_type=MESH,
        ).wait_recv()
    for copy in norm_copies:
        copy.wait_send()
    store.wait()
    whole = jnp.zeros(tile, jnp.float32)
    for d in range(n_gx):
        whole = whole + xsum[d]
    cells = float(nx * ny * nz * n_gx * group)
    whole = jnp.sum(whole, axis=1, keepdims=True) / cells
    norm_out[...] = jnp.broadcast_to(jnp.sqrt(whole), tile)


def finish(pieces, norms, pot, rows, pot_out, rows_out, norm_out, pot_buf, rows_buf, in_sem, out_sem):
    parts = []
    for k, (source, buf, target) in enumerate(((rows, rows_buf, rows_out), (pot, pot_buf, pot_out))):
        count = source.shape[0] // pieces
        for i in range(pieces):
            at = pl.ds(i * count, count)
            n = k * pieces + i
            parts.append(
                (
                    pltpu.make_async_copy(source.at[at], buf.at[at], in_sem.at[n]),
                    pltpu.make_async_copy(buf.at[at], target.at[at], out_sem.at[n]),
                )
            )
    for load, _ in parts:
        load.start()
    for k in range(CYCLES):
        norm_out[k] = norms[k, 0]
    for load, store in parts:
        load.wait()
        store.start()
    for _, store in parts:
        store.wait()


def to_rows(a):
    slots, fine = a.shape
    return a.reshape(slots, fine // LANES, LANES).transpose(1, 0, 2).reshape(slots * fine // LANES, LANES)


def from_rows(a, slots):
    return a.reshape(-1, slots, LANES).transpose(1, 0, 2).reshape(slots, -1)


def local(sizes, c_src, c_shift, c_start, f_src, f_shift, f_start, corner, owner):
    n_gx, n_gy, n_gz = sizes
    group = n_gy * n_gz
    slots = owner.shape[1]
    nx, ny, nz = c_src.shape
    fine = f_src.shape[1]
    f32 = jnp.float32
    face_rows = ny // min(ny // 8, LANES // nx)
    vmem = pl.BlockSpec(memory_space=pltpu.VMEM)
    smem = pl.BlockSpec(memory_space=pltpu.SMEM)
    dma = pltpu.SemaphoreType.DMA
    pot, rows, norms = pl.pallas_call(
        functools.partial(kernel, sizes),
        out_shape=(
            jax.ShapeDtypeStruct((nx, ny, nz), f32),
            jax.ShapeDtypeStruct((slots * fine // LANES, LANES), f32),
            jax.ShapeDtypeStruct((8, LANES), f32),
        ),
        in_specs=[smem, smem] + [pl.BlockSpec(memory_space=pl.ANY)] * 6,
        out_specs=(pl.BlockSpec(memory_space=pl.ANY), vmem, vmem),
        scratch_shapes=[
            pltpu.VMEM((nx, ny, nz), f32),
            pltpu.VMEM((nx, ny, nz), f32),
            pltpu.VMEM((slots * fine // LANES, LANES), f32),
            pltpu.VMEM((slots * fine // LANES, LANES), f32),
            pltpu.VMEM((slots * fine // LANES, LANES), f32),
            dma((6,)),
            pltpu.VMEM((2, nx + 2, ny, nz), f32),
            pltpu.VMEM((nx, ny, nz), f32),
            pltpu.VMEM((nx, ny, nz), f32),
            pltpu.VMEM((2, 2, nx, nz), f32),
            pltpu.VMEM((2, nx, nz), f32),
            pltpu.VMEM((2, 2, face_rows, nz), f32),
            pltpu.VMEM((2, face_rows, nz), f32),
            pltpu.VMEM((2, slots, (SIDE + 2) * 8, LANES), f32),
            pltpu.VMEM((slots, SIDE, 8, LANES), f32),
            pltpu.VMEM((slots, SIDE, 8, LANES), f32),
            pltpu.VMEM((slots, SIDE, 8, LANES), f32),
            pltpu.VMEM((2, slots, FOOT, 8, LANES), f32),
            pltpu.VMEM((slots, 32, LANES), f32),
            pltpu.VMEM((slots, 32, LANES), f32),
            pltpu.VMEM((group, 40, LANES), f32),
            pltpu.VMEM((group, 40, LANES), f32),
            pltpu.VMEM((group, 32, LANES), f32),
            pltpu.VMEM((group, 32, LANES), f32),
            pltpu.VMEM((group, 8, LANES), f32),
            pltpu.VMEM((CYCLES, 8, LANES), f32),
            pltpu.VMEM((n_gx, 8, LANES), f32),
            dma((group,)),
            dma((group,)),
            dma((group,)),
            dma((group,)),
            dma((2, 6)),
            dma((2, 6)),
            dma((n_gx,)),
            dma((n_gx,)),
        ],
        compiler_params=pltpu.CompilerParams(collective_id=0, has_side_effects=True),
    )(corner.transpose(2, 0, 1), owner, c_src, c_shift, c_start, to_rows(f_src), to_rows(f_shift), to_rows(f_start))
    pieces = 2
    anywhere = pl.BlockSpec(memory_space=pl.ANY)
    pot, rows, norms = pl.pallas_call(
        functools.partial(finish, pieces),
        out_shape=(
            jax.ShapeDtypeStruct(pot.shape, f32),
            jax.ShapeDtypeStruct(rows.shape, f32),
            jax.ShapeDtypeStruct((CYCLES,), f32),
        ),
        in_specs=[smem, anywhere, anywhere],
        out_specs=(anywhere, anywhere, smem),
        scratch_shapes=[
            pltpu.VMEM(pot.shape, f32),
            pltpu.VMEM(rows.shape, f32),
            dma((2 * pieces,)),
            dma((2 * pieces,)),
        ],
    )(norms, pot, rows)
    return pot, from_rows(rows, slots), norms


def solution(mesh):
    sizes = (mesh.shape["gx"], mesh.shape["gy"], mesh.shape["gz"])
    everywhere = ("gx", "gy", "gz")
    block = P(*everywhere)
    in_specs = (
        block,
        block,
        block,
        P(everywhere, None),
        P(everywhere, None),
        P(everywhere, None),
        P(everywhere, None, None),
        P(everywhere, None),
    )
    out_specs = (block, P(everywhere, None), P())
    return jax.shard_map(
        functools.partial(local, sizes), mesh=mesh, in_specs=in_specs, out_specs=out_specs, check_vma=False
    )
```

profile of v0, /device:TPU:0, one launch (start us, length us, event | category | flops | bytes accessed | tf_op | source)
XLA Modules:
  0.0 66.9 jit_solution(6241702339213888570)
XLA Ops:
  0.6 63.1 %shard_map.103 = (f32[16,32,128]{2,1,0:T(8,128)}, f32[1024,128]{1,0:T(8,128)}, f32[8,128]{1,0:T(8,128)}) custom-call(s32[3,1,4]{2,1,0:T(1,128)} %bitcast.24, s32[1,4]{1,0:T(1,128)} %owner.1, f32[16,32,128]{2,1,0:T(8,128)} %c_src_hbm.1, f32[16,32,128]{2,1,0:T(8,128)} %c_shift_hbm.1, f32[16,32,128]{2,1,0:T(8,128)} %c_start_hbm.1, f32[1024,128]{1,0:T(8,128)} %bitcast.21, ...), custom_call_target="tpu_custom_call" | custom-call | tf_op jit(solution)/shard_map/pallas_call | solution.py:618
  63.8 3.1 %shard_map.104 = (f32[16,32,128]{2,1,0:T(8,128)}, f32[1024,128]{1,0:T(8,128)}, f32[2]{0:T(128)}) custom-call(f32[8,128]{1,0:T(8,128)} %get-tuple-element.9.norms, f32[16,32,128]{2,1,0:T(8,128)} %get-tuple-element.10.pot, f32[1024,128]{1,0:T(8,128)} %get-tuple-element.11.rows), custom_call_target="tpu_custom_call" | custom-call | tf_op jit(solution)/shard_map/pallas_call | solution.py:668
where the time goes:
time: 67.1 us; the launch traced here: 66.9 us
  Pallas kernels  66.3 us (99%)
    pallas_call x1, Pallas kernels, local(): pl.pallas_call(functools.partial(kernel, sizes), out_shape=(jax.ShapeDtyp...  63.1 us
    pallas_call x1, Pallas kernels, local(): pl.pallas_call(functools.partial(finish, pieces), out_shape=(jax.ShapeDty...  3.13 us

commit v1 on v0

--- a/solution.py
+++ b/solution.py
@@ -513,8 +513,8 @@
         if cycle < CYCLES - 1:
             send_faces(0)
 
-    store = pltpu.make_async_copy(U.at[0, pl.ds(1, nx)], pot_out, in_sem.at[0])
-    store.start()
+    for x in range(nx):
+        pot_out[x] = U[0, x + 1]
 
     for copy in return_copies:
         copy.wait_send()
@@ -562,7 +562,6 @@
         ).wait_recv()
     for copy in norm_copies:
         copy.wait_send()
-    store.wait()
     whole = jnp.zeros(tile, jnp.float32)
     for d in range(n_gx):
         whole = whole + xsum[d]
@@ -571,27 +570,13 @@
     norm_out[...] = jnp.broadcast_to(jnp.sqrt(whole), tile)
 
 
-def finish(pieces, norms, pot, rows, pot_out, rows_out, norm_out, pot_buf, rows_buf, in_sem, out_sem):
-    parts = []
-    for k, (source, buf, target) in enumerate(((rows, rows_buf, rows_out), (pot, pot_buf, pot_out))):
-        count = source.shape[0] // pieces
-        for i in range(pieces):
-            at = pl.ds(i * count, count)
-            n = k * pieces + i
-            parts.append(
-                (
-                    pltpu.make_async_copy(source.at[at], buf.at[at], in_sem.at[n]),
-                    pltpu.make_async_copy(buf.at[at], target.at[at], out_sem.at[n]),
-                )
-            )
-    for load, _ in parts:
-        load.start()
+def finish(norms, pot, rows, pot_out, rows_out, norm_out, sem):
+    stores = [pltpu.make_async_copy(pot, pot_out, sem.at[0]), pltpu.make_async_copy(rows, rows_out, sem.at[1])]
+    for store in stores:
+        store.start()
     for k in range(CYCLES):
         norm_out[k] = norms[k, 0]
-    for load, store in parts:
-        load.wait()
-        store.start()
-    for _, store in parts:
+    for store in stores:
         store.wait()
 
 
@@ -618,12 +603,12 @@
     pot, rows, norms = pl.pallas_call(
         functools.partial(kernel, sizes),
         out_shape=(
-            jax.ShapeDtypeStruct((nx, ny, nz), f32),
-            jax.ShapeDtypeStruct((slots * fine // LANES, LANES), f32),
-            jax.ShapeDtypeStruct((8, LANES), f32),
+            pltpu.VMEM((nx, ny, nz), f32),
+            pltpu.VMEM((slots * fine // LANES, LANES), f32),
+            pltpu.VMEM((8, LANES), f32),
         ),
         in_specs=[smem, smem] + [pl.BlockSpec(memory_space=pl.ANY)] * 6,
-        out_specs=(pl.BlockSpec(memory_space=pl.ANY), vmem, vmem),
+        out_specs=(vmem, vmem, vmem),
         scratch_shapes=[
             pltpu.VMEM((nx, ny, nz), f32),
             pltpu.VMEM((nx, ny, nz), f32),
@@ -661,25 +646,20 @@
             dma((n_gx,)),
             dma((n_gx,)),
         ],
-        compiler_params=pltpu.CompilerParams(collective_id=0, has_side_effects=True),
+        compiler_params=pltpu.CompilerParams(collective_id=0, has_side_effects=True, vmem_limit_bytes=63000000),
     )(corner.transpose(2, 0, 1), owner, c_src, c_shift, c_start, to_rows(f_src), to_rows(f_shift), to_rows(f_start))
-    pieces = 2
     anywhere = pl.BlockSpec(memory_space=pl.ANY)
     pot, rows, norms = pl.pallas_call(
-        functools.partial(finish, pieces),
+        finish,
         out_shape=(
             jax.ShapeDtypeStruct(pot.shape, f32),
             jax.ShapeDtypeStruct(rows.shape, f32),
             jax.ShapeDtypeStruct((CYCLES,), f32),
         ),
-        in_specs=[smem, anywhere, anywhere],
+        in_specs=[smem, vmem, vmem],
         out_specs=(anywhere, anywhere, smem),
-        scratch_shapes=[
-            pltpu.VMEM(pot.shape, f32),
-            pltpu.VMEM(rows.shape, f32),
-            dma((2 * pieces,)),
-            dma((2 * pieces,)),
-        ],
+        scratch_shapes=[dma((2,))],
+        compiler_params=pltpu.CompilerParams(vmem_limit_bytes=8 << 20),
     )(norms, pot, rows)
     return pot, from_rows(rows, slots), norms
 

time: 67.1 us -> 65.3 us (0.973)
  Pallas kernels: 66.3 us -> 64.5 us
    pallas_call x2, Pallas kernels: 66.3 us -> 64.5 us  [the longest x1 62.5 us: local(): pl.pallas_call(functools.partial(kernel, sizes), out_shape=(pltpu.VMEM((n...]
where the time goes in v1:
time: 65.3 us; the launch traced here: 65.1 us
  Pallas kernels  64.5 us (99%)
    pallas_call x1, Pallas kernels, local(): pl.pallas_call(functools.partial(kernel, sizes), out_shape=(pltpu.VMEM((n...  62.5 us
    pallas_call x1, Pallas kernels, local(): pl.pallas_call(finish, out_shape=(jax.ShapeDtypeStruct(pot.shape, f32), j...  2.01 us

profile of v1, /device:TPU:0, one launch (start us, length us, event | category | flops | bytes accessed | tf_op | source)
XLA Modules:
  0.0 65.1 jit_solution(14325298930809369134)
XLA Ops:
  0.6 62.5 %shard_map.103 = (f32[16,32,128]{2,1,0:T(8,128)S(1)}, f32[1024,128]{1,0:T(8,128)S(1)}, f32[8,128]{1,0:T(8,128)S(1)}) custom-call(s32[3,1,4]{2,1,0:T(1,128)} %bitcast.24, s32[1,4]{1,0:T(1,128)} %owner.1, f32[16,32,128]{2,1,0:T(8,128)} %c_src_hbm.1, f32[16,32,128]{2,1,0:T(8,128)} %c_shift_hbm.1, f32[16,32,128]{2,1,0:T(8,128)} %c_start_hbm.1, ...), custom_call_target="tpu_custom_call" | custom-call | tf_op jit(solution)/shard_map/pallas_call | solution.py:603
  63.1 2.0 %shard_map.104 = (f32[16,32,128]{2,1,0:T(8,128)}, f32[1024,128]{1,0:T(8,128)}, f32[2]{0:T(128)}) custom-call(f32[8,128]{1,0:T(8,128)S(1)} %get-tuple-element.9.norms, f32[16,32,128]{2,1,0:T(8,128)S(1)} %get-tuple-element.10.pot, f32[1024,128]{1,0:T(8,128)S(1)} %get-tuple-element.11.rows), custom_call_target="tpu_custom_call" | custom-call | tf_op jit(solution)/shard_map/pallas_call | solution.py:652

commit v2 on v1

v2 whole, which is shorter than its diff:
```python
import functools
import itertools

import jax
import jax.numpy as jnp
from jax import lax
from jax.experimental import pallas as pl
from jax.experimental.pallas import tpu as pltpu
from jax.sharding import PartitionSpec as P

FOOT = 16
CYCLES = 2
CSWEEPS = 4
FSWEEPS = 3
OMEGA = 0.8
KEEP = 1.0 - OMEGA
MESH = pl.DeviceIdType.MESH
LANES = 128
SIDE = 2 * FOOT
DEEP = CSWEEPS
PAD = 8
DIRS = [d for d in itertools.product((-1, 0, 1), repeat=3) if any(d)]
FPLANE = SIDE + 8


def take(x, idx):
    return jnp.take_along_axis(x, idx, axis=1, mode="promise_in_bounds")


def iota(shape, dim):
    return lax.broadcasted_iota(jnp.int32, shape, dim)


def turn(x, by):
    by = by % LANES
    return pltpu.roll(x, by, 1) if by else x


def kernel(
    sizes,
    corner,
    owner,
    c_src_hbm,
    c_shift_hbm,
    c_start_hbm,
    f_src_hbm,
    f_shift_hbm,
    f_start_hbm,
    pot_out,
    fine_out,
    norm_out,
    c_shift,
    f_src,
    f_shift,
    f_start,
    in_sem,
    P0,
    P1,
    W0,
    W1,
    C0,
    C1,
    E0,
    A0,
    A1,
    B0,
    B1,
    Q0,
    Q1,
    pk,
    zs,
    V0,
    V1,
    T,
    FW,
    FS,
    FD,
    G,
    PRE,
    compact,
    R,
    pout,
    prec,
    rout,
    rrec,
    slotid,
    sums,
    xsum,
    gsum,
    p_send,
    p_recv,
    r_send,
    r_recv,
    h_send,
    h_recv,
    n_send,
    n_recv,
    g_send,
    g_recv,
):
    n_gx, n_gy, n_gz = sizes
    group = n_gy * n_gz
    slots = owner.shape[1]
    nx, ny, nz = c_src_hbm.shape
    along_y = ny // FOOT
    first, rows = PAD + 8, ny + 16
    inner, block = pl.ds(first, ny), pl.ds(PAD, rows)
    inside = pl.ds(DEEP, nx)
    gx, gy, gz = lax.axis_index("gx"), lax.axis_index("gy"), lax.axis_index("gz")
    me = gy * n_gz + gz
    V = (V0, V1)
    zero_rows = jnp.zeros((rows, LANES), jnp.float32)
    zero_tile = jnp.zeros((8, LANES), jnp.float32)

    def rank_id(rank):
        return (gx, rank // n_gz, rank % n_gz)

    loads = [
        pltpu.make_async_copy(source, target, in_sem.at[i])
        for i, (source, target) in enumerate(
            (
                (c_start_hbm, P0.at[inside, inner]),
                (c_shift_hbm, c_shift),
                (c_src_hbm, C0.at[inside, inner]),
                (f_start_hbm, f_start),
                (f_src_hbm, f_src),
                (f_shift_hbm, f_shift),
            )
        )
    ]
    for load in loads:
        load.start()

    for F in (P0, W0, C0, E0):
        for X in range(nx + 2 * DEEP):
            if DEEP <= X < DEEP + nx:
                F[X, pl.ds(PAD, 8)] = zero_tile
                F[X, pl.ds(first + ny, 8)] = zero_tile
            else:
                F[X, block] = zero_rows
    for f in range(4):
        for a in range(3):
            for b in range(2):
                zs[f, a, b] = zero_rows

    barrier = pltpu.get_barrier_semaphore()
    greeted = group - 1 + n_gx - 1
    for d in range(1, group):
        pl.semaphore_signal(barrier, inc=1, device_id=rank_id((me + d) % group), device_id_type=MESH)
    for d in range(1, n_gx):
        pl.semaphore_signal(barrier, inc=1, device_id=((gx + d) % n_gx, gy, gz), device_id_type=MESH)
    for dx, dy, dz in DIRS:
        if dx and (dy or dz):
            other = ((gx + dx + n_gx) % n_gx, (gy + dy + n_gy) % n_gy, (gz + dz + n_gz) % n_gz)
            pl.semaphore_signal(barrier, inc=1, device_id=other, device_id_type=MESH)
            greeted += 1

    tile = (8, LANES)
    lane = iota(tile, 1)
    part = lane // SIDE
    box_row = []
    box_col = []
    box_live = []
    for s in range(slots):
        box_row.append((corner[1, 0, s] // 2 - gy * ny) // FOOT)
        box_col.append((corner[2, 0, s] // 2 - gz * nz) // FOOT)
        box_live.append(owner[0, s] < group)

    def exchange(out, rec, send, recv, count):
        copies = []
        for d in range(1, group):
            peer = (me + d) % group
            copy = pltpu.make_async_remote_copy(
                src_ref=out.at[peer, pl.ds(0, count)],
                dst_ref=rec.at[me, pl.ds(0, count)],
                send_sem=send.at[d],
                recv_sem=recv.at[d],
                device_id=rank_id(peer),
                device_id_type=MESH,
            )
            copy.start()
            copies.append(copy)
        rec[me, pl.ds(0, count)] = out[me, pl.ds(0, count)]
        return copies

    def arrive(out, rec, send, recv, count):
        for d in range(1, group):
            source = (me + group - d) % group
            pltpu.make_async_remote_copy(
                src_ref=out.at[source, pl.ds(0, count)],
                dst_ref=rec.at[source, pl.ds(0, count)],
                send_sem=send.at[d],
                recv_sem=recv.at[d],
                device_id=rank_id(source),
                device_id_type=MESH,
            ).wait_recv()

    def pack_parents():
        for m in range(FOOT // 4):
            for s in range(slots):
                idx = box_col[s] * FOOT + (lane % FOOT)
                acc = jnp.zeros(tile, jnp.float32)
                for k in range(4):
                    for h in range(2):
                        X = DEEP + 4 * m + k
                        a = P0[X, pl.ds(first + 8 * h, 8)]
                        for b in range(1, along_y):
                            other = P0[X, pl.ds(first + FOOT * b + 8 * h, 8)]
                            a = jnp.where(box_row[s] == b, other, a)
                        acc = jnp.where(lane // FOOT == 2 * k + h, take(a, idx), acc)
                compact[s, pl.ds(8 * m, 8), :] = acc

        for q in range(group):
            acc = jnp.zeros((32, LANES), jnp.float32)
            for s in range(slots):
                acc = jnp.where(owner[0, s] == q, compact[s], acc)
            pout[q, pl.ds(0, 32)] = acc

    def pack_flags():
        for q in range(group):
            flag = zero_tile
            for s in range(slots):
                flag = jnp.where(owner[0, s] == q, 1.0, flag)
            pout[q, pl.ds(32, 8)] = flag

    def slot_masks():
        count = zero_tile
        for q in range(group):
            flag = prec[q, pl.ds(32, 8)]
            slotid[q] = jnp.where(flag > 0.5, count, -1.0)
            count = count + flag
        return count

    def ghosts(par):
        for m in range(FOOT // 4):
            at = pl.ds(8 * m, 8)
            tiles = []
            for j in range(slots):
                acc = zero_tile
                for q in range(group):
                    acc = jnp.where(slotid[q] == float(j), prec[q, at], acc)
                tiles.append(acc)
            for k in range(4):
                for h in range(2):
                    idx = k * 32 + h * FOOT + (lane % SIDE) // 2
                    acc = take(tiles[0], idx)
                    for j in range(1, slots):
                        acc = jnp.where(part == j, take(tiles[j], idx), acc)
                    for e in range(2):
                        G[par, 4 * m + k, pl.ds(2 * 8 * h + e, 8, stride=2), :] = acc

    wide = (SIDE, LANES)
    z_pos = iota(wide, 1) % SIDE

    def start_of(x):
        return 8 + (x + 1) * FPLANE

    def edges(par):
        for v in V:
            v[pl.ds(start_of(-1), SIDE)] = G[par, 0]
            v[pl.ds(start_of(SIDE), SIDE)] = G[par, FOOT - 1]
            for X in range(FOOT):
                low = G[par, X, pl.ds(0, 1)]
                top = G[par, X, pl.ds(SIDE - 1, 1)]
                for e in range(2):
                    v[pl.ds(start_of(2 * X + e) - 1, 1)] = low
                    v[pl.ds(start_of(2 * X + e) + SIDE, 1)] = top

    def beside_fine(v, par, x):
        at = start_of(x)
        u = v[pl.ds(at, SIDE)]
        ghost = G[par, x // 2]
        zu = jnp.where(z_pos < SIDE - 1, turn(u, -1), ghost)
        zl = jnp.where(z_pos > 0, turn(u, 1), ghost)
        across = v[pl.ds(at + FPLANE, SIDE)] + v[pl.ds(at - FPLANE, SIDE)]
        along = v[pl.ds(at + 1, SIDE)] + v[pl.ds(at - 1, SIDE)]
        return u, (across + along) + (zu + zl)

    def fine_sweep(vp, par):
        for x in range(SIDE):
            u, s = beside_fine(V[vp], par, x)
            V[1 - vp][pl.ds(start_of(x), SIDE)] = KEEP * u + FW[x] * (FS[x] + s)

    def fine_remainder(vp, par):
        total = jnp.zeros(wide, jnp.float32)
        for X in range(FOOT):
            t = None
            for e in range(2):
                x = 2 * X + e
                u, s = beside_fine(V[vp], par, x)
                r = (FS[x] - FD[x] * u) + s
                total = total + r * r
                t = r if t is None else t + r
            T[X] = t + turn(t, -1)
        square = zero_tile
        for g in range(SIDE // 8):
            square = square + total[8 * g : 8 * g + 8]
        return square

    def shrink():
        for m in range(FOOT // 4):
            packed = []
            for k in range(4):
                X = 4 * m + k
                halves = []
                for h in range(2):
                    even = T[X, pl.ds(16 * h, 8, stride=2), :]
                    odd = T[X, pl.ds(16 * h + 1, 8, stride=2), :]
                    halves.append(even + odd)
                packed.append(jnp.where(lane % 2 == 0, halves[0], turn(halves[1], 1)) * 0.125)
            for j in range(slots):
                acc = turn(packed[0], -SIDE * j)
                for k in range(1, 4):
                    acc = jnp.where(part == k, turn(packed[k], SIDE * (k - j)), acc)
                R[j, pl.ds(8 * m, 8)] = acc

    def pack_returns():
        for q in range(group):
            which = slotid[q]
            for m in range(FOOT // 4):
                at = pl.ds(m * 8, 8)
                acc = zero_tile
                for j in range(slots):
                    acc = jnp.where(which == float(j), R[j, at], acc)
                rout[q, at] = acc

    def deposit():
        for m in range(FOOT // 4):
            tiles = []
            for s in range(slots):
                tiles.append(rrec[jnp.minimum(owner[0, s], group - 1), pl.ds(8 * m, 8)])
            for k in range(4):
                X = DEEP + 4 * m + k
                for h in range(2):
                    idx = k * 32 + (lane % FOOT) * 2 + h
                    got = []
                    for s in range(slots):
                        col = jnp.where(box_live[s], box_col[s], -1)
                        got.append(jnp.where(lane // FOOT == col, take(tiles[s], idx), 0.0))
                    for b in range(along_y):
                        acc = jnp.where(box_row[0] == b, got[0], 0.0)
                        for s in range(1, slots):
                            acc = acc + jnp.where(box_row[s] == b, got[s], 0.0)
                        E0[X, pl.ds(first + FOOT * b + 8 * h, 8)] = acc

    tall = iota((ny, LANES), 1)

    def pack_lanes(F, f):
        acc = turn(F[DEEP, inner], DEEP)
        for x in range(1, nx):
            acc = jnp.where(tall // (2 * DEEP) == x, turn(F[DEEP + x, inner], 2 * DEEP * x + DEEP), acc)
        pk[f] = acc

    def regions(F, f, depth, d):
        dx, dy, dz = d
        x_src = {0: inside, -1: pl.ds(DEEP, depth), 1: pl.ds(DEEP + nx - depth, depth)}[dx]
        x_dst = {0: inside, -1: pl.ds(DEEP + nx, depth), 1: pl.ds(DEEP - depth, depth)}[dx]
        if dz == 0:
            y_src = {0: inner, -1: pl.ds(first, 8), 1: pl.ds(first + ny - 8, 8)}[dy]
            y_dst = {0: inner, -1: pl.ds(first + ny, 8), 1: pl.ds(PAD, 8)}[dy]
            return F.at[x_src, y_src], F.at[x_dst, y_dst]
        y_src = {0: pl.ds(0, ny), -1: pl.ds(0, 8), 1: pl.ds(ny - 8, 8)}[dy]
        y_dst = {0: pl.ds(8, ny), -1: pl.ds(8 + ny, 8), 1: pl.ds(0, 8)}[dy]
        return pk.at[f, y_src], zs.at[f, {0: 0, -1: 1, 1: 2}[dx], 0 if dz < 0 else 1, y_dst]

    def there(d):
        tests = []
        for step, at, count in zip(d, (gx, gy, gz), sizes):
            if step < 0:
                tests.append(at > 0)
            if step > 0:
                tests.append(at < count - 1)
        return functools.reduce(jnp.logical_and, tests)

    def halo_copy(F, f, depth, i):
        d = DIRS[i]
        source, target = regions(F, f, depth, d)
        return pltpu.make_async_remote_copy(
            src_ref=source,
            dst_ref=target,
            send_sem=h_send.at[f, i],
            recv_sem=h_recv.at[f, len(DIRS) - 1 - i],
            device_id=(gx + d[0], gy + d[1], gz + d[2]),
            device_id_type=MESH,
        )

    def halo_wait(F, f, depth, i):
        d = DIRS[i]
        _, target = regions(F, f, depth, tuple(-v for v in d))
        return pltpu.make_async_remote_copy(
            src_ref=target,
            dst_ref=target,
            send_sem=h_send.at[f, i],
            recv_sem=h_recv.at[f, i],
            device_id=(gx + d[0], gy + d[1], gz + d[2]),
            device_id_type=MESH,
        )

    far_first = sorted(range(len(DIRS)), key=lambda i: -sum(map(abs, DIRS[i])))

    def send_halo(F, f, depth):
        pack_lanes(F, f)
        for i in far_first:
            pl.when(there(DIRS[i]))(halo_copy(F, f, depth, i).start)

    def wait_halo(F, f, depth):
        for i in reversed(far_first):

            @pl.when(there(DIRS[i]))
            def _():
                halo_copy(F, f, depth, i).wait_send()
                halo_wait(F, f, depth, i).wait_recv()

    low_part = iota((rows, LANES), 1) % (2 * DEEP) >= DEEP

    def lane_halo(f, depth):
        merged = [jnp.where(low_part, zs[f, a, 0], zs[f, a, 1]) for a in range(3)]
        for X in range(DEEP - depth, DEEP + nx + depth):
            if X < DEEP:
                a, i = 2, nx - DEEP + X
            elif X < DEEP + nx:
                a, i = 0, X - DEEP
            else:
                a, i = 1, X - DEEP - nx
            yield X, turn(merged[a], -(2 * DEEP * i + DEEP))

    def unpack_lanes(f, F1):
        for X, value in lane_halo(f, DEEP):
            F1[X, block] = value

    def sweep(source, target, comp, depth, squares=False):
        U0, U1 = source
        count = rows if depth else ny
        off = PAD if depth else first
        here, up, down = pl.ds(off, count), pl.ds(off + 1, count), pl.ds(off - 1, count)
        wlane = iota((count, LANES), 1)
        left, right = wlane == 0, wlane == LANES - 1
        total = jnp.zeros((count, LANES), jnp.float32)
        for X in range(DEEP - depth, DEEP + nx + depth):
            u = (U0[X, here], U1[X, here])
            prev = [turn(v, 1) for v in u]
            nxt = [turn(v, -1) for v in u]
            for t in range(2 if depth else 1):
                U = source[t]
                z = jnp.where(left, prev[1 - t], prev[t]) + jnp.where(right, nxt[1 - t], nxt[t])
                s = ((U[X - 1, here] + U[X + 1, here]) + (U[X, up] + U[X, down])) + z
                s = s + comp[t][X, here]
                target[t][X, here] = KEEP * u[t] + (W0, W1)[t][X, here] * s
                if squares:
                    last = s - (6.0 + c_shift[X - DEEP]) * u[t]
                    total = total + last * last
        return total

    def add_deposit(X, at, t, e):
        A, W, C, Q = ((A0, W0, C0, Q0), (A1, W1, C1, Q1))[t]
        A[X, at] = A[X, at] + W[X, at] * e
        Q[X, at] = C[X, at] + e

    loads[0].wait()
    pack_parents()
    pack_flags()
    loads[1].wait()
    for x in range(nx):
        W0[DEEP + x, inner] = OMEGA / (6.0 + c_shift[x])
    pl.semaphore_wait(barrier, greeted)
    parent_copies = exchange(pout, prec, p_send, p_recv, 40)
    send_halo(P0, 0, DEEP)
    send_halo(W0, 1, DEEP - 1)
    loads[2].wait()
    send_halo(C0, 2, DEEP - 1)

    for load in loads[3:]:
        load.wait()

    def spread(a, x):
        parts = [a[pl.ds(x * 8 * slots + j, 8, stride=slots), :] for j in range(slots)]
        result = []
        for w in range(SIDE // 8):
            acc = turn(parts[0], -SIDE * w)
            for j in range(1, slots):
                acc = jnp.where(part == j, turn(parts[j], SIDE * (j - w)), acc)
            result.append(acc)
        return result

    def gather(parts):
        result = []
        for j in range(slots):
            acc = turn(parts[0], -SIDE * j)
            for w in range(1, SIDE // 8):
                acc = jnp.where(part == w, turn(parts[w], SIDE * (w - j)), acc)
            result.append(acc)
        return result

    def prepare():
        @pl.loop(0, SIDE, unroll=4)
        def _(x):
            for w, value in enumerate(spread(f_start, x)):
                V0[pl.ds(8 + (x + 1) * FPLANE + w, 8, stride=4), :] = value
            for w, value in enumerate(spread(f_src, x)):
                FS[x, pl.ds(w, 8, stride=4), :] = value
            for w, value in enumerate(spread(f_shift, x)):
                diagonal = 6.0 + value
                FD[x, pl.ds(w, 8, stride=4), :] = diagonal
                FW[x, pl.ds(w, 8, stride=4), :] = OMEGA / diagonal

    prepare()

    vp = 0
    return_copies = []
    for cycle in range(CYCLES):
        par = cycle % 2
        arrive(pout, prec, p_send, p_recv, 32 if cycle else 40)
        if cycle == 0:
            count = slot_masks()
            occupied = [count > float(j) for j in range(slots)]
            live_lanes = count > part.astype(jnp.float32)
        ghosts(par)
        if cycle > 0:
            for x in range(SIDE):
                at = pl.ds(start_of(x), SIDE)
                V[vp][at] = V[vp][at] + (G[par, x // 2] - G[1 - par, x // 2])
        edges(par)
        for _ in range(FSWEEPS):
            fine_sweep(vp, par)
            vp = 1 - vp
        square = jnp.where(live_lanes, fine_remainder(vp, par), 0.0)
        shrink()
        for copy in return_copies:
            copy.wait_send()
        pack_returns()
        return_copies = exchange(rout, rrec, r_send, r_recv, 32)
        wait_halo(P0, 0, DEEP)
        unpack_lanes(0, P1)
        if cycle == 0:
            wait_halo(W0, 1, DEEP - 1)
            unpack_lanes(1, W1)
            wait_halo(C0, 2, DEEP - 1)
            unpack_lanes(2, C1)
        sweep((P0, P1), (A0, A1), (C0, C1), DEEP - 1)
        arrive(rout, rrec, r_send, r_recv, 32)
        deposit()
        send_halo(E0, 3, DEEP - 1)
        for x in range(nx):
            add_deposit(DEEP + x, inner, 0, E0[DEEP + x, inner])
        wait_halo(E0, 3, DEEP - 1)
        for X in range(1, nx + 2 * DEEP - 1):
            if DEEP <= X < DEEP + nx:
                for at in (pl.ds(PAD, 8), pl.ds(first + ny, 8)):
                    add_deposit(X, at, 0, E0[X, at])
            else:
                add_deposit(X, block, 0, E0[X, block])
        for X, value in lane_halo(3, DEEP - 1):
            add_deposit(X, block, 1, value)
        now, later = (A0, A1), (B0, B1)
        for depth in range(CSWEEPS - 2, 0, -1):
            sweep(now, later, (Q0, Q1), depth)
            now, later = later, now
        total = sweep(now, (P0, None), (Q0, None), 0, True)
        for g in range(ny // 8):
            square = square + total[8 * g : 8 * g + 8]
        sums[cycle] = square
        for copy in parent_copies:
            copy.wait_send()
        if cycle == CYCLES - 1:
            xsum[gx] = jnp.where(
                iota(tile, 0) == 0,
                jnp.sum(sums[0], axis=0, keepdims=True),
                jnp.where(iota(tile, 0) == 1, jnp.sum(sums[1], axis=0, keepdims=True), 0.0),
            )
            norm_copies = []
            for d in range(1, n_gx):
                copy = pltpu.make_async_remote_copy(
                    src_ref=xsum.at[gx],
                    dst_ref=xsum.at[gx],
                    send_sem=n_send.at[d],
                    recv_sem=n_recv.at[d],
                    device_id=((gx + d) % n_gx, gy, gz),
                    device_id_type=MESH,
                )
                copy.start()
                norm_copies.append(copy)
        pack_parents()
        parent_copies = exchange(pout, prec, p_send, p_recv, 32)
        if cycle < CYCLES - 1:
            send_halo(P0, 0, DEEP)

    par = CYCLES % 2
    for x in range(nx):
        pot_out[x] = P0[DEEP + x, inner]

    def settle():
        @pl.loop(0, FOOT, unroll=4)
        def _(X):
            for e in range(2):
                x = 2 * X + e
                parts = []
                for w in range(SIDE // 8):
                    old = G[1 - par, X, pl.ds(w, 8, stride=4), :]
                    parts.append(V[vp][pl.ds(8 + (x + 1) * FPLANE + w, 8, stride=4), :] - old)
                for j, value in enumerate(gather(parts)):
                    PRE[x, j] = value

    settle()
    for d in range(1, n_gx):
        source = (gx + n_gx - d) % n_gx
        pltpu.make_async_remote_copy(
            src_ref=xsum.at[source],
            dst_ref=xsum.at[source],
            send_sem=n_send.at[d],
            recv_sem=n_recv.at[d],
            device_id=(source, gy, gz),
            device_id_type=MESH,
        ).wait_recv()
    for copy in norm_copies:
        copy.wait_send()
    mine = zero_tile
    for d in range(n_gx):
        mine = mine + xsum[d]
    gsum[me] = mine
    group_copies = []
    for d in range(1, group):
        copy = pltpu.make_async_remote_copy(
            src_ref=gsum.at[me],
            dst_ref=gsum.at[me],
            send_sem=g_send.at[d],
            recv_sem=g_recv.at[d],
            device_id=rank_id((me + d) % group),
            device_id_type=MESH,
        )
        copy.start()
        group_copies.append(copy)

    for copy in return_copies:
        copy.wait_send()
    arrive(pout, prec, p_send, p_recv, 32)
    for copy in parent_copies:
        copy.wait_send()
    ghosts(par)

    def deliver():
        @pl.loop(0, FOOT, unroll=4)
        def _(X):
            parts = [G[par, X, pl.ds(w, 8, stride=4), :] for w in range(SIDE // 8)]
            for j, value in enumerate(gather(parts)):
                for e in range(2):
                    x = 2 * X + e
                    place = pl.ds(x * 8 * slots + j, 8, stride=slots)
                    fine_out[place, :] = jnp.where(occupied[j], PRE[x, j] + value, 0.0)

    deliver()
    for d in range(1, group):
        source = (me + group - d) % group
        pltpu.make_async_remote_copy(
            src_ref=gsum.at[source],
            dst_ref=gsum.at[source],
            send_sem=g_send.at[d],
            recv_sem=g_recv.at[d],
            device_id=rank_id(source),
            device_id_type=MESH,
        ).wait_recv()
    for copy in group_copies:
        copy.wait_send()
    whole = zero_tile
    for q in range(group):
        whole = whole + gsum[q]
    cells = float(nx * ny * nz * n_gx * group)
    whole = jnp.sum(whole, axis=1, keepdims=True) / cells
    norm_out[...] = jnp.broadcast_to(jnp.sqrt(whole), tile)


def finish(norms, pot, rows, pot_out, rows_out, norm_out, sem):
    stores = [pltpu.make_async_copy(pot, pot_out, sem.at[0]), pltpu.make_async_copy(rows, rows_out, sem.at[1])]
    for store in stores:
        store.start()
    for k in range(CYCLES):
        norm_out[k] = norms[k, 0]
    for store in stores:
        store.wait()


def to_rows(a):
    slots, fine = a.shape
    return a.reshape(slots, fine // LANES, LANES).transpose(1, 0, 2).reshape(slots * fine // LANES, LANES)


def from_rows(a, slots):
    return a.reshape(-1, slots, LANES).transpose(1, 0, 2).reshape(slots, -1)


def local(sizes, c_src, c_shift, c_start, f_src, f_shift, f_start, corner, owner):
    n_gx, n_gy, n_gz = sizes
    group = n_gy * n_gz
    slots = owner.shape[1]
    nx, ny, nz = c_src.shape
    fine = f_src.shape[1]
    f32 = jnp.float32
    assert 2 * DEEP * nx == LANES == nz and slots * SIDE == LANES and nx == FOOT
    vmem = pl.BlockSpec(memory_space=pltpu.VMEM)
    smem = pl.BlockSpec(memory_space=pltpu.SMEM)
    anywhere = pl.BlockSpec(memory_space=pl.ANY)
    dma = pltpu.SemaphoreType.DMA
    rows = pltpu.VMEM((slots * fine // LANES, LANES), f32)
    ring = pltpu.VMEM((nx + 2 * DEEP, ny + 5 * 8, LANES), f32)
    box = pltpu.VMEM((8 + (SIDE + 2) * FPLANE + 8, LANES), f32)
    planes = pltpu.VMEM((SIDE, SIDE, LANES), f32)
    pot, fine_rows, norms = pl.pallas_call(
        functools.partial(kernel, sizes),
        out_shape=(pltpu.VMEM((nx, ny, nz), f32), rows, pltpu.VMEM((8, LANES), f32)),
        in_specs=[smem, smem] + [anywhere] * 6,
        out_specs=(vmem, vmem, vmem),
        scratch_shapes=[pltpu.VMEM((nx, ny, nz), f32), rows, rows, rows, dma((6,))]
        + [ring] * 13
        + [
            pltpu.VMEM((4, ny, LANES), f32),
            pltpu.VMEM((4, 3, 2, ny + 16, LANES), f32),
            box,
            box,
            pltpu.VMEM((FOOT, SIDE, LANES), f32),
            planes,
            planes,
            planes,
            pltpu.VMEM((2, FOOT, SIDE, LANES), f32),
            pltpu.VMEM((SIDE, slots, 8, LANES), f32),
            pltpu.VMEM((slots, 32, LANES), f32),
            pltpu.VMEM((slots, 32, LANES), f32),
            pltpu.VMEM((group, 40, LANES), f32),
            pltpu.VMEM((group, 40, LANES), f32),
            pltpu.VMEM((group, 32, LANES), f32),
            pltpu.VMEM((group, 32, LANES), f32),
            pltpu.VMEM((group, 8, LANES), f32),
            pltpu.VMEM((CYCLES, 8, LANES), f32),
            pltpu.VMEM((n_gx, 8, LANES), f32),
            pltpu.VMEM((group, 8, LANES), f32),
            dma((group,)),
            dma((group,)),
            dma((group,)),
            dma((group,)),
            dma((4, len(DIRS))),
            dma((4, len(DIRS))),
            dma((n_gx,)),
            dma((n_gx,)),
            dma((group,)),
            dma((group,)),
        ],
        compiler_params=pltpu.CompilerParams(collective_id=0, has_side_effects=True, vmem_limit_bytes=63000000),
    )(corner.transpose(2, 0, 1), owner, c_src, c_shift, c_start, to_rows(f_src), to_rows(f_shift), to_rows(f_start))
    pot, fine_rows, norms = pl.pallas_call(
        finish,
        out_shape=(
            jax.ShapeDtypeStruct(pot.shape, f32),
            jax.ShapeDtypeStruct(fine_rows.shape, f32),
            jax.ShapeDtypeStruct((CYCLES,), f32),
        ),
        in_specs=[smem, vmem, vmem],
        out_specs=(anywhere, anywhere, smem),
        scratch_shapes=[dma((2,))],
        compiler_params=pltpu.CompilerParams(vmem_limit_bytes=8 << 20),
    )(norms, pot, fine_rows)
    return pot, from_rows(fine_rows, slots), norms


def solution(mesh):
    sizes = (mesh.shape["gx"], mesh.shape["gy"], mesh.shape["gz"])
    everywhere = ("gx", "gy", "gz")
    block = P(*everywhere)
    in_specs = (
        block,
        block,
        block,
        P(everywhere, None),
        P(everywhere, None),
        P(everywhere, None),
        P(everywhere, None, None),
        P(everywhere, None),
    )
    out_specs = (block, P(everywhere, None), P())
    return jax.shard_map(
        functools.partial(local, sizes), mesh=mesh, in_specs=in_specs, out_specs=out_specs, check_vma=False
    )
```

time: 65.3 us -> 52.4 us (0.80)
  Pallas kernels: 64.5 us -> 51.6 us
    pallas_call x1, Pallas kernels: 62.5 us -> 49.6 us  [local(): pl.pallas_call(functools.partial(kernel, sizes), out_shape=(pltpu.VMEM((n...]
where the time goes in v2:
time: 52.4 us; the launch traced here: 52.2 us
  Pallas kernels  51.6 us (98%)
  between operations  0.64 us (1%)
    pallas_call x1, Pallas kernels, local(): pl.pallas_call(functools.partial(kernel, sizes), out_shape=(pltpu.VMEM((n...  49.6 us
    pallas_call x1, Pallas kernels, local(): pl.pallas_call(finish, out_shape=(jax.ShapeDtypeStruct(pot.shape, f32), j...  2.01 us

profile of v2, /device:TPU:0, one launch (start us, length us, event | category | flops | bytes accessed | tf_op | source)
XLA Modules:
  0.0 52.2 jit_solution(8811218087760187291)
XLA Ops:
  0.6 49.6 %shard_map.103 = (f32[16,32,128]{2,1,0:T(8,128)S(1)}, f32[1024,128]{1,0:T(8,128)S(1)}, f32[8,128]{1,0:T(8,128)S(1)}) custom-call(s32[3,1,4]{2,1,0:T(1,128)} %bitcast.24, s32[1,4]{1,0:T(1,128)} %owner.1, f32[16,32,128]{2,1,0:T(8,128)} %c_src_hbm.1, f32[16,32,128]{2,1,0:T(8,128)} %c_shift_hbm.1, f32[16,32,128]{2,1,0:T(8,128)} %c_start_hbm.1, ...), custom_call_target="tpu_custom_call" | custom-call | tf_op jit(solution)/shard_map/pallas_call | solution.py:706
  50.2 2.0 %shard_map.104 = (f32[16,32,128]{2,1,0:T(8,128)}, f32[1024,128]{1,0:T(8,128)}, f32[2]{0:T(128)}) custom-call(f32[8,128]{1,0:T(8,128)S(1)} %get-tuple-element.9.norms, f32[16,32,128]{2,1,0:T(8,128)S(1)} %get-tuple-element.10.pot, f32[1024,128]{1,0:T(8,128)S(1)} %get-tuple-element.11.rows), custom_call_target="tpu_custom_call" | custom-call | tf_op jit(solution)/shard_map/pallas_call | solution.py:747

commit v3 on v2

v3 whole, which is shorter than its diff:
```python
import functools
import itertools
import math

import jax
import jax.numpy as jnp
from jax import lax
from jax.experimental import pallas as pl
from jax.experimental.pallas import tpu as pltpu
from jax.sharding import PartitionSpec as P

FOOT = 16
CYCLES = 2
CSWEEPS = 4
FSWEEPS = 3
OMEGA = 0.8
KEEP = 1.0 - OMEGA
MESH = pl.DeviceIdType.MESH
LANES = 128
SIDE = 2 * FOOT
DEEP = CSWEEPS
PAD = 8
CH = 16
PIECES = 2
FCH = 16
DIRS = [d for d in itertools.product((-1, 0, 1), repeat=3) if any(d)]
FPLANE = SIDE + 8


def take(x, idx):
    return jnp.take_along_axis(x, idx, axis=1, mode="promise_in_bounds")


def iota(shape, dim):
    return lax.broadcasted_iota(jnp.int32, shape, dim)


def turn(x, by):
    by = by % LANES
    return pltpu.roll(x, by, 1) if by else x


def kernel(
    sizes,
    corner_hbm,
    owner_hbm,
    c_src_hbm,
    c_shift_hbm,
    c_start_hbm,
    f_src_hbm,
    f_shift_hbm,
    f_start_hbm,
    pot_out,
    fine_out,
    norm_out,
    corner,
    owner,
    c_src,
    c_shift,
    f_src,
    f_shift,
    f_start,
    in_sem,
    H0,
    P1,
    W1,
    A0,
    A1,
    B0,
    B1,
    Q1,
    pk,
    zs,
    V0,
    V1,
    T,
    FW,
    FS,
    FD,
    G,
    PRE,
    compact,
    R,
    pout,
    prec,
    rout,
    rrec,
    slotid,
    sums,
    own,
    team,
    xsum,
    gsum,
    p_sem,
    r_sem,
    h_send,
    h_recv,
    n_sem,
    g_sem,
):
    n_gx, n_gy, n_gz = sizes
    group = n_gy * n_gz
    devices = n_gx * group
    direct = devices <= 64
    slots = owner_hbm.shape[1]
    nx, ny, nz = c_src_hbm.shape
    along_y = ny // FOOT
    first, rows = PAD + 8, ny + 16
    inner, block = pl.ds(first, ny), pl.ds(PAD, rows)
    inside = pl.ds(DEEP, nx)
    gx, gy, gz = lax.axis_index("gx"), lax.axis_index("gy"), lax.axis_index("gz")
    me = gy * n_gz + gz
    V = (V0, V1)
    P0, W0, E0 = (H0.at[f] for f in range(3))
    zero_rows = jnp.zeros((rows, LANES), jnp.float32)
    zero_tile = jnp.zeros((8, LANES), jnp.float32)

    def rank_id(rank):
        return (gx, rank // n_gz, rank % n_gz)

    loads = [
        pltpu.make_async_copy(source, target, in_sem.at[i])
        for i, (source, target) in enumerate(
            (
                (c_start_hbm, H0.at[0, inside, inner]),
                (c_shift_hbm, c_shift),
                (c_src_hbm, c_src),
                (f_start_hbm, f_start),
                (f_src_hbm, f_src),
                (f_shift_hbm, f_shift),
                (corner_hbm, corner),
                (owner_hbm, owner),
            )
        )
    ]
    for load in (loads[0], loads[6], loads[7]):
        load.start()

    barrier = pltpu.get_barrier_semaphore()
    greeted = 0
    for a, b, c in itertools.product(range(n_gx), range(n_gy), range(n_gz)):
        near = [min(v, n - v) for v, n in zip((a, b, c), sizes)]
        if any(near) and (direct or a == 0 or (b == 0 and c == 0) or max(near) == 1):
            other = ((gx + a) % n_gx, (gy + b) % n_gy, (gz + c) % n_gz)
            pl.semaphore_signal(barrier, inc=1, device_id=other, device_id_type=MESH)
            greeted += 1

    for load in loads[1:6]:
        load.start()

    tile = (8, LANES)
    lane = iota(tile, 1)
    part = lane // SIDE
    def exchange(out, rec, sems, count):
        for d in range(1, group):
            peer = (me + d) % group
            pltpu.make_async_remote_copy(
                src_ref=out.at[peer, pl.ds(0, count)],
                dst_ref=rec.at[me, pl.ds(0, count)],
                send_sem=sems.at[0],
                recv_sem=sems.at[1],
                device_id=rank_id(peer),
                device_id_type=MESH,
            ).start()
        rec[me, pl.ds(0, count)] = out[me, pl.ds(0, count)]

    def all_of(out, rec, sems, count):
        most = pl.ds(0, group - 1)
        return pltpu.make_async_remote_copy(
            src_ref=out.at[most, pl.ds(0, count)],
            dst_ref=rec.at[most, pl.ds(0, count)],
            send_sem=sems.at[0],
            recv_sem=sems.at[1],
            device_id=rank_id((me + 1) % group),
            device_id_type=MESH,
        )

    def pack_parents():
        for s in range(slots):
            idx = box_col[s] * FOOT + (lane % FOOT)
            for m in range(FOOT // 4):
                acc = jnp.zeros(tile, jnp.float32)
                for k in range(4):
                    for h in range(2):
                        X = DEEP + 4 * m + k
                        a = P0[X, pl.ds(first + 8 * h, 8)]
                        for b in range(1, along_y):
                            other = P0[X, pl.ds(first + FOOT * b + 8 * h, 8)]
                            a = jnp.where(box_row[s] == b, other, a)
                        acc = jnp.where(lane // FOOT == 2 * k + h, take(a, idx), acc)
                compact[s, pl.ds(8 * m, 8), :] = acc

        for q in range(group):
            acc = jnp.zeros((32, LANES), jnp.float32)
            for s in range(slots):
                acc = jnp.where(owner[0, s] == q, compact[s], acc)
            pout[q, pl.ds(0, 32)] = acc

    def pack_flags():
        for q in range(group):
            flag = zero_tile
            for s in range(slots):
                flag = jnp.where(owner[0, s] == q, 1.0, flag)
            pout[q, pl.ds(32, 8)] = flag

    def slot_masks():
        count = zero_tile
        for q in range(group):
            flag = prec[q, pl.ds(32, 8)]
            slotid[q] = jnp.where(flag > 0.5, count, -1.0)
            count = count + flag
        return count

    def ghosts(par):
        tiles = []
        for m in range(FOOT // 4):
            at = pl.ds(8 * m, 8)
            for j in range(slots):
                acc = zero_tile
                for q in range(group):
                    acc = jnp.where(slotid[q] == float(j), prec[q, at], acc)
                tiles.append(acc)
        for k in range(4):
            for h in range(2):
                idx = k * 32 + h * FOOT + (lane % SIDE) // 2
                for m in range(FOOT // 4):
                    acc = take(tiles[m * slots], idx)
                    for j in range(1, slots):
                        acc = jnp.where(part == j, take(tiles[m * slots + j], idx), acc)
                    for e in range(2):
                        G[par, 4 * m + k, pl.ds(2 * 8 * h + e, 8, stride=2), :] = acc

    wide = (FCH, LANES)
    z_pos = iota(wide, 1) % SIDE

    def start_of(x):
        return 8 + (x + 1) * FPLANE

    def edges(par):
        for v in V:
            v[pl.ds(start_of(-1), SIDE)] = G[par, 0]
            v[pl.ds(start_of(SIDE), SIDE)] = G[par, FOOT - 1]
            for X in range(FOOT):
                low = G[par, X, pl.ds(0, 1)]
                top = G[par, X, pl.ds(SIDE - 1, 1)]
                for e in range(2):
                    v[pl.ds(start_of(2 * X + e) - 1, 1)] = low
                    v[pl.ds(start_of(2 * X + e) + SIDE, 1)] = top

    def beside_fine(v, par, x, r):
        at = start_of(x) + r
        u = v[pl.ds(at, FCH)]
        ghost = G[par, x // 2, pl.ds(r, FCH)]
        zu = jnp.where(z_pos < SIDE - 1, turn(u, -1), ghost)
        zl = jnp.where(z_pos > 0, turn(u, 1), ghost)
        across = v[pl.ds(at + FPLANE, FCH)] + v[pl.ds(at - FPLANE, FCH)]
        along = v[pl.ds(at + 1, FCH)] + v[pl.ds(at - 1, FCH)]
        return u, (across + along) + (zu + zl)

    def fine_sweep(vp, par):
        for x in range(SIDE):
            for r in range(0, SIDE, FCH):
                at = pl.ds(r, FCH)
                u, s = beside_fine(V[vp], par, x, r)
                V[1 - vp][pl.ds(start_of(x) + r, FCH)] = KEEP * u + FW[x, at] * (FS[x, at] + s)

    def fine_remainder(vp, par):
        total = jnp.zeros(wide, jnp.float32)
        for X in range(FOOT):
            for r in range(0, SIDE, FCH):
                at = pl.ds(r, FCH)
                t = None
                for e in range(2):
                    x = 2 * X + e
                    u, s = beside_fine(V[vp], par, x, r)
                    w = (FS[x, at] - FD[x, at] * u) + s
                    total = total + w * w
                    t = w if t is None else t + w
                T[X, at] = t
        square = zero_tile
        for g in range(FCH // 8):
            square = square + total[8 * g : 8 * g + 8]
        return square

    def shrink():
        for m in range(FOOT // 4):
            packed = []
            for k in range(4):
                X = 4 * m + k
                halves = []
                for h in range(2):
                    even = T[X, pl.ds(16 * h, 8, stride=2), :]
                    odd = T[X, pl.ds(16 * h + 1, 8, stride=2), :]
                    both = even + odd
                    halves.append(both + turn(both, -1))
                packed.append(jnp.where(lane % 2 == 0, halves[0], turn(halves[1], 1)) * 0.125)
            for j in range(slots):
                acc = turn(packed[0], -SIDE * j)
                for k in range(1, 4):
                    acc = jnp.where(part == k, turn(packed[k], SIDE * (k - j)), acc)
                R[j, pl.ds(8 * m, 8)] = acc

    def pack_returns():
        for q in range(group):
            which = slotid[q]
            for m in range(FOOT // 4):
                at = pl.ds(m * 8, 8)
                acc = zero_tile
                for j in range(slots):
                    acc = jnp.where(which == float(j), R[j, at], acc)
                rout[q, at] = acc

    def deposit():
        cols = [jnp.where(box_live[s], box_col[s], -1) for s in range(slots)]
        tiles = []
        for m in range(FOOT // 4):
            for s in range(slots):
                tiles.append(rrec[jnp.minimum(owner[0, s], group - 1), pl.ds(8 * m, 8)])
        for k in range(4):
            for h in range(2):
                idx = k * 32 + (lane % FOOT) * 2 + h
                for m in range(FOOT // 4):
                    got = []
                    for s in range(slots):
                        got.append(jnp.where(lane // FOOT == cols[s], take(tiles[m * slots + s], idx), 0.0))
                    for b in range(along_y):
                        x, y = 4 * m + k, FOOT * b + 8 * h
                        acc = c_src[x, pl.ds(y, 8)]
                        for s in range(slots):
                            acc = acc + jnp.where(box_row[s] == b, got[s], 0.0)
                        E0[DEEP + x, pl.ds(first + y, 8)] = acc

    def spread_row(row, received, sems, peers):
        for d, to in enumerate(peers):
            pltpu.make_async_remote_copy(
                src_ref=row,
                dst_ref=received.at[d],
                send_sem=sems.at[0],
                recv_sem=sems.at[1],
                device_id=to,
                device_id_type=MESH,
            ).start()

    def add_rows(row, received, sems):
        wait = pltpu.make_async_remote_copy(
            src_ref=received,
            dst_ref=received,
            send_sem=sems.at[0],
            recv_sem=sems.at[1],
            device_id=rank_id((me + 1) % group),
            device_id_type=MESH,
        )
        wait.wait_recv()
        wait.wait_send()
        total = row[...]
        for d in range(received.shape[0]):
            total = total + received[d]
        return total

    tall = iota((ny, LANES), 1)

    def pack_lanes(F, f):
        acc = turn(F[DEEP, inner], DEEP)
        for x in range(1, nx):
            acc = jnp.where(tall // (2 * DEEP) == x, turn(F[DEEP + x, inner], 2 * DEEP * x + DEEP), acc)
        pk[f] = acc

    def regions(fields, depth, d):
        dx, dy, dz = d
        x_src = {0: inside, -1: pl.ds(DEEP, depth), 1: pl.ds(DEEP + nx - depth, depth)}[dx]
        x_dst = {0: inside, -1: pl.ds(DEEP + nx, depth), 1: pl.ds(DEEP - depth, depth)}[dx]
        if dz == 0:
            y_src = {0: inner, -1: pl.ds(first, 8), 1: pl.ds(first + ny - 8, 8)}[dy]
            y_dst = {0: inner, -1: pl.ds(first + ny, 8), 1: pl.ds(PAD, 8)}[dy]
            return H0.at[fields, x_src, y_src], H0.at[fields, x_dst, y_dst]
        y_src = {0: pl.ds(0, ny), -1: pl.ds(0, 8), 1: pl.ds(ny - 8, 8)}[dy]
        y_dst = {0: pl.ds(8, ny), -1: pl.ds(8 + ny, 8), 1: pl.ds(0, 8)}[dy]
        return pk.at[fields, y_src], zs.at[fields, {0: 0, -1: 1, 1: 2}[dx], 0 if dz < 0 else 1, y_dst]

    def there(d):
        tests = []
        for step, at, count in zip(d, (gx, gy, gz), sizes):
            if step < 0:
                tests.append(at > 0)
            if step > 0:
                tests.append(at < count - 1)
        return functools.reduce(jnp.logical_and, tests)

    def flag(d):
        return tuple(abs(v) if n == 2 else v for v, n in zip(d, sizes))

    flags = sorted({flag(d) for d in DIRS})

    def halo_copy(kind, fields, depth, i):
        d = DIRS[i]
        source, target = regions(fields, depth, d)
        return pltpu.make_async_remote_copy(
            src_ref=source,
            dst_ref=target,
            send_sem=h_send.at[flags.index(flag(d))],
            recv_sem=h_recv.at[kind, flags.index(flag(tuple(-v for v in d)))],
            device_id=(gx + d[0], gy + d[1], gz + d[2]),
            device_id_type=MESH,
        )

    def halo_wait(kind, fields, depth, i):
        d = DIRS[i]
        _, target = regions(fields, depth, tuple(-v for v in d))
        return pltpu.make_async_remote_copy(
            src_ref=target,
            dst_ref=target,
            send_sem=h_send.at[flags.index(flag(d))],
            recv_sem=h_recv.at[kind, flags.index(flag(d))],
            device_id=(gx + d[0], gy + d[1], gz + d[2]),
            device_id_type=MESH,
        )

    def clear_halos():
        for d in DIRS:

            @pl.when(jnp.logical_not(there(d)))
            def _():
                _, target = regions(pl.ds(0, 3), DEEP, tuple(-v for v in d))
                target[...] = jnp.zeros(target.shape, jnp.float32)

    far_first = sorted(range(len(DIRS)), key=lambda i: -sum(map(abs, DIRS[i])))
    flat = [i for i in far_first if DIRS[i][2] == 0]
    packed = [i for i in far_first if DIRS[i][2] != 0]
    planes = [i for i in flat if DIRS[i][1] == 0]
    others = [i for i in far_first if i not in planes]

    def send_halo(kind, fields, depth, which):
        for i in which:
            pl.when(there(DIRS[i]))(halo_copy(kind, fields, depth, i).start)

    def wait_halo(kind, fields, depth):
        for i in reversed(far_first):

            @pl.when(there(DIRS[i]))
            def _():
                halo_copy(kind, fields, depth, i).wait_send()
                halo_wait(kind, fields, depth, i).wait_recv()

    both, only_start, only_composite = pl.ds(0, 2), pl.ds(0, 1), pl.ds(2, 1)

    low_part = iota((rows, LANES), 1) % (2 * DEEP) >= DEEP

    def lane_halo(f, depth):
        merged = [jnp.where(low_part, zs[f, a, 0], zs[f, a, 1]) for a in range(3)]
        for X in range(DEEP - depth, DEEP + nx + depth):
            if X < DEEP:
                a, i = 2, nx - DEEP + X
            elif X < DEEP + nx:
                a, i = 0, X - DEEP
            else:
                a, i = 1, X - DEEP - nx
            yield X, turn(merged[a], -(2 * DEEP * i + DEEP))

    def unpack_lanes(f, F1):
        for X, value in lane_halo(f, DEEP):
            F1[X, block] = value

    def reach(depth):
        for X in range(DEEP - depth, DEEP + nx + depth):
            left = depth - max(DEEP - X, X - (DEEP + nx - 1), 0)
            for r in range(PAD, PAD + rows, 8):
                rest = left - (0 if first <= r < first + ny else 1)
                if rest >= 0:
                    yield X, r, 2 if rest else 1

    lane0, lane127 = lane == 0, lane == LANES - 1

    def sweep(source, target, comp, depth, squares=False):
        U0, U1 = source
        total = zero_tile
        for X, r, tiles in reach(depth):
            here, up, down = pl.ds(r, 8), pl.ds(r + 1, 8), pl.ds(r - 1, 8)
            u = (U0[X, here], U1[X, here])
            prev = [turn(v, 1) for v in u]
            nxt = [turn(v, -1) for v in u]
            for t in range(tiles):
                U = source[t]
                z = jnp.where(lane0, prev[1 - t], prev[t]) + jnp.where(lane127, nxt[1 - t], nxt[t])
                s = ((U[X - 1, here] + U[X + 1, here]) + (U[X, up] + U[X, down])) + z
                if comp is not None:
                    s = s + comp[t][X, here]
                target[t][X, here] = KEEP * u[t] + (W0, W1)[t][X, here] * s
                if squares:
                    last = s - (6.0 + c_shift[X - DEEP, pl.ds(r - first, 8)]) * u[t]
                    total = total + last * last
        return total

    def inner_composite():
        for x in range(nx):
            X = DEEP + x
            A0[X, inner] = A0[X, inner] + W0[X, inner] * E0[X, inner]

    def outer_composite():
        values = dict(lane_halo(2, DEEP - 1))
        for X, r, tiles in reach(DEEP - 1):
            at = pl.ds(r, 8)
            inside_block = DEEP <= X < DEEP + nx and first <= r < first + ny
            if not inside_block:
                A0[X, at] = A0[X, at] + W0[X, at] * E0[X, at]
            if tiles == 2:
                value = values[X][r - PAD : r - PAD + 8]
                Q1[X, at] = value
                A1[X, at] = A1[X, at] + W1[X, at] * value

    loads[6].wait()
    loads[7].wait()
    box_row = []
    box_col = []
    box_live = []
    for s in range(slots):
        box_row.append((corner[1, 0, s] // 2 - gy * ny) // FOOT)
        box_col.append((corner[2, 0, s] // 2 - gz * nz) // FOOT)
        box_live.append(owner[0, s] < group)
    loads[0].wait()
    pack_parents()
    pack_flags()
    pl.semaphore_wait(barrier, greeted)
    exchange(pout, prec, p_sem, 40)
    clear_halos()
    for load in loads[1:6]:
        load.wait()
    for x in range(nx):
        W0[DEEP + x, inner] = OMEGA / (6.0 + c_shift[x])
    send_halo(0, both, DEEP, planes)

    def spread(a, x):
        parts = [a[pl.ds(x * 8 * slots + j, 8, stride=slots), :] for j in range(slots)]
        result = []
        for w in range(SIDE // 8):
            acc = turn(parts[0], -SIDE * w)
            for j in range(1, slots):
                acc = jnp.where(part == j, turn(parts[j], SIDE * (j - w)), acc)
            result.append(acc)
        return result

    def gather(parts):
        result = []
        for j in range(slots):
            acc = turn(parts[0], -SIDE * j)
            for w in range(1, SIDE // 8):
                acc = jnp.where(part == w, turn(parts[w], SIDE * (w - j)), acc)
            result.append(acc)
        return result

    def prepare():
        @pl.loop(0, SIDE, unroll=4)
        def _(x):
            for w, value in enumerate(spread(f_start, x)):
                V0[pl.ds(8 + (x + 1) * FPLANE + w, 8, stride=4), :] = value
            for w, value in enumerate(spread(f_src, x)):
                FS[x, pl.ds(w, 8, stride=4), :] = value
            for w, value in enumerate(spread(f_shift, x)):
                diagonal = 6.0 + value
                FD[x, pl.ds(w, 8, stride=4), :] = diagonal
                FW[x, pl.ds(w, 8, stride=4), :] = OMEGA / diagonal

    prepare()
    pack_lanes(P0, 0)
    pack_lanes(W0, 1)
    send_halo(0, both, DEEP, others)

    vp = 0
    for cycle in range(CYCLES):
        par = cycle % 2
        parents = all_of(pout, prec, p_sem, 32 if cycle else 40)
        parents.wait_recv()
        if cycle > 0:
            send_halo(0, only_start, DEEP, others)
        if cycle == 0:
            count = slot_masks()
            occupied = [count > float(j) for j in range(slots)]
            live_lanes = count > part.astype(jnp.float32)
        ghosts(par)
        if cycle > 0:
            for x in range(SIDE):
                at = pl.ds(start_of(x), SIDE)
                V[vp][at] = V[vp][at] + (G[par, x // 2] - G[1 - par, x // 2])
        edges(par)
        for _ in range(FSWEEPS):
            fine_sweep(vp, par)
            vp = 1 - vp
        square = jnp.where(live_lanes, fine_remainder(vp, par), 0.0)
        shrink()
        returns = all_of(rout, rrec, r_sem, 32)
        if cycle > 0:
            returns.wait_send()
        pack_returns()
        exchange(rout, rrec, r_sem, 32)
        wait_halo(0, only_start if cycle else both, DEEP)
        unpack_lanes(0, P1)
        if cycle == 0:
            unpack_lanes(1, W1)
        sweep((P0, P1), (A0, A1), None, DEEP - 1)
        returns.wait_recv()
        deposit()
        pack_lanes(E0, 2)
        send_halo(1, only_composite, DEEP - 1, far_first)
        inner_composite()
        wait_halo(1, only_composite, DEEP - 1)
        outer_composite()
        now, later = (A0, A1), (B0, B1)
        for depth in range(CSWEEPS - 2, 0, -1):
            sweep(now, later, (E0, Q1), depth)
            now, later = later, now
        total = sweep(now, (P0, None), (E0, None), 0, True)
        sums[cycle] = square + total
        parents.wait_send()
        if cycle == CYCLES - 1:
            halves = []
            for k in range(2):
                row = jnp.sum(sums[k], axis=0, keepdims=True)
                halves.append(row + turn(row, LANES // 2))
            own[...] = jnp.where(iota((1, LANES), 1) < LANES // 2, halves[0], halves[1])
            peers = []
            for a, b, c in itertools.product(range(n_gx), range(n_gy), range(n_gz)):
                if (a or b or c) and (direct or (b == 0 and c == 0)):
                    peers.append(((gx + a) % n_gx, (gy + b) % n_gy, (gz + c) % n_gz))
            spread_row(own, xsum, n_sem, peers)
        pack_parents()
        exchange(pout, prec, p_sem, 32)
        if cycle < CYCLES - 1:
            send_halo(0, only_start, DEEP, planes)
            pack_lanes(P0, 0)

    par = CYCLES % 2
    for x in range(nx):
        pot_out[x] = P0[DEEP + x, inner]

    def settle():
        @pl.loop(0, FOOT, unroll=4)
        def _(X):
            for e in range(2):
                x = 2 * X + e
                parts = []
                for w in range(SIDE // 8):
                    old = G[1 - par, X, pl.ds(w, 8, stride=4), :]
                    parts.append(V[vp][pl.ds(8 + (x + 1) * FPLANE + w, 8, stride=4), :] - old)
                for j, value in enumerate(gather(parts)):
                    PRE[x, j] = value

    settle()
    if not direct:
        team[...] = add_rows(own, xsum, n_sem)
        spread_row(team, gsum, g_sem, [rank_id((me + d) % group) for d in range(1, group)])

    returns.wait_send()
    parents = all_of(pout, prec, p_sem, 32)
    parents.wait_recv()
    parents.wait_send()
    ghosts(par)

    def deliver():
        for X in range(FOOT):
            parts = [G[par, X, pl.ds(w, 8, stride=4), :] for w in range(SIDE // 8)]
            for j, value in enumerate(gather(parts)):
                for e in range(2):
                    x = 2 * X + e
                    place = pl.ds(x * 8 * slots + j, 8, stride=slots)
                    fine_out[place, :] = jnp.where(occupied[j], PRE[x, j] + value, 0.0)

    deliver()
    whole = add_rows(own, xsum, n_sem) if direct else add_rows(team, gsum, g_sem)
    cells = float(nx * ny * nz * devices)
    mine = (lane >= LANES // 2) == (iota(tile, 0) > 0)
    both = jnp.where(mine, jnp.broadcast_to(whole, tile), 0.0)
    norm_out[...] = jnp.broadcast_to(jnp.sqrt(jnp.sum(both, axis=1, keepdims=True) / cells), tile)


def finish(norms, pot, rows, pot_out, rows_out, norm_out, held, sem):
    load = pltpu.make_async_copy(norms, held, sem.at[0])
    stores = [load]
    for k, (source, target) in enumerate(((rows, rows_out), (pot, pot_out))):
        count = source.shape[0] // PIECES
        for i in range(PIECES):
            at = pl.ds(i * count, count)
            stores.append(pltpu.make_async_copy(source.at[at], target.at[at], sem.at[1 + k * PIECES + i]))
    for store in stores:
        store.start()
    load.wait()
    for k in range(CYCLES):
        norm_out[k] = held[k, 0]
    for store in stores[1:]:
        store.wait()


def to_rows(a):
    slots, fine = a.shape
    return a.reshape(slots, fine // LANES, LANES).transpose(1, 0, 2).reshape(slots * fine // LANES, LANES)


def from_rows(a, slots):
    return a.reshape(-1, slots, LANES).transpose(1, 0, 2).reshape(slots, -1)


def local(sizes, c_src, c_shift, c_start, f_src, f_shift, f_start, corner, owner):
    n_gx, n_gy, n_gz = sizes
    group = n_gy * n_gz
    slots = owner.shape[1]
    nx, ny, nz = c_src.shape
    fine = f_src.shape[1]
    f32 = jnp.float32
    devices = n_gx * group
    direct = devices <= 64
    flags = math.prod(2 if n == 2 else 3 for n in sizes) - 1
    assert 2 * DEEP * nx == LANES == nz and slots * SIDE == LANES and nx == FOOT
    vmem = pl.BlockSpec(memory_space=pltpu.VMEM)
    smem = pl.BlockSpec(memory_space=pltpu.SMEM)
    anywhere = pl.BlockSpec(memory_space=pl.ANY)
    dma = pltpu.SemaphoreType.DMA
    rows = pltpu.VMEM((slots * fine // LANES, LANES), f32)
    ring = pltpu.VMEM((nx + 2 * DEEP, ny + 5 * 8, LANES), f32)
    box = pltpu.VMEM((8 + (SIDE + 2) * FPLANE + 8, LANES), f32)
    planes = pltpu.VMEM((SIDE, SIDE, LANES), f32)
    pot, fine_rows, norms = pl.pallas_call(
        functools.partial(kernel, sizes),
        out_shape=(pltpu.VMEM((nx, ny, nz), f32), rows, pltpu.VMEM((8, LANES), f32)),
        in_specs=[anywhere] * 8,
        out_specs=(vmem, vmem, vmem),
        scratch_shapes=[
            pltpu.SMEM((3, 1, slots), jnp.int32),
            pltpu.SMEM((1, slots), jnp.int32),
            pltpu.VMEM((nx, ny, nz), f32),
            pltpu.VMEM((nx, ny, nz), f32),
            rows,
            rows,
            rows,
            dma((8,)),
        ]
        + [pltpu.VMEM((3,) + ring.shape, f32)]
        + [ring] * 7
        + [
            pltpu.VMEM((3, ny, LANES), f32),
            pltpu.VMEM((3, 3, 2, ny + 16, LANES), f32),
            box,
            box,
            pltpu.VMEM((FOOT, SIDE, LANES), f32),
            planes,
            planes,
            planes,
            pltpu.VMEM((2, FOOT, SIDE, LANES), f32),
            pltpu.VMEM((SIDE, slots, 8, LANES), f32),
            pltpu.VMEM((slots, 32, LANES), f32),
            pltpu.VMEM((slots, 32, LANES), f32),
            pltpu.VMEM((group, 40, LANES), f32),
            pltpu.VMEM((group, 40, LANES), f32),
            pltpu.VMEM((group, 32, LANES), f32),
            pltpu.VMEM((group, 32, LANES), f32),
            pltpu.VMEM((group, 8, LANES), f32),
            pltpu.VMEM((CYCLES, 8, LANES), f32),
            pltpu.VMEM((1, LANES), f32),
            pltpu.VMEM((1, LANES), f32),
            pltpu.VMEM(((devices if direct else n_gx) - 1, 1, LANES), f32),
            pltpu.VMEM((group - 1, 1, LANES), f32),
            dma((2,)),
            dma((2,)),
            dma((flags,)),
            dma((2, flags)),
            dma((2,)),
            dma((2,)),
        ],
        compiler_params=pltpu.CompilerParams(collective_id=0, has_side_effects=True, vmem_limit_bytes=63000000),
    )(corner.transpose(2, 0, 1), owner, c_src, c_shift, c_start, to_rows(f_src), to_rows(f_shift), to_rows(f_start))
    pot, fine_rows, norms = pl.pallas_call(
        finish,
        out_shape=(
            jax.ShapeDtypeStruct(pot.shape, f32),
            jax.ShapeDtypeStruct(fine_rows.shape, f32),
            jax.ShapeDtypeStruct((CYCLES,), f32),
        ),
        in_specs=[vmem, vmem, vmem],
        out_specs=(anywhere, anywhere, smem),
        scratch_shapes=[pltpu.SMEM((8, LANES), f32), dma((1 + 2 * PIECES,))],
        compiler_params=pltpu.CompilerParams(vmem_limit_bytes=8 << 20),
    )(norms, pot, fine_rows)
    return pot, from_rows(fine_rows, slots), norms


def solution(mesh):
    sizes = (mesh.shape["gx"], mesh.shape["gy"], mesh.shape["gz"])
    everywhere = ("gx", "gy", "gz")
    block = P(*everywhere)
    in_specs = (
        block,
        block,
        block,
        P(everywhere, None),
        P(everywhere, None),
        P(everywhere, None),
        P(everywhere, None, None),
        P(everywhere, None),
    )
    out_specs = (block, P(everywhere, None), P())
    return jax.shard_map(
        functools.partial(local, sizes), mesh=mesh, in_specs=in_specs, out_specs=out_specs, check_vma=False
    )
```

time: 52.4 us -> 43.7 us (0.83)
  Pallas kernels: 51.6 us -> 42.9 us
    pallas_call x1, Pallas kernels: 49.6 us -> 41.5 us  [local(): pl.pallas_call(functools.partial(kernel, sizes), out_shape=(pltpu.VMEM((n...]
    pallas_call x1, Pallas kernels: 2.01 us -> 1.43 us  [local(): pl.pallas_call(finish, out_shape=(jax.ShapeDtypeStruct(pot.shape, f32), j...]
where the time goes in v3:
time: 43.7 us; the launch traced here: 43.5 us
  Pallas kernels  42.9 us (98%)
  between operations  0.64 us (1%)
    pallas_call x1, Pallas kernels, local(): pl.pallas_call(functools.partial(kernel, sizes), out_shape=(pltpu.VMEM((n...  41.5 us
    pallas_call x1, Pallas kernels, local(): pl.pallas_call(finish, out_shape=(jax.ShapeDtypeStruct(pot.shape, f32), j...  1.43 us

profile of v3, /device:TPU:0, one launch (start us, length us, event | category | flops | bytes accessed | tf_op | source)
XLA Modules:
  0.0 43.5 jit_solution(883187748782802354)
XLA Ops:
  0.6 41.5 %shard_map.103 = (f32[16,32,128]{2,1,0:T(8,128)S(1)}, f32[1024,128]{1,0:T(8,128)S(1)}, f32[8,128]{1,0:T(8,128)S(1)}) custom-call(s32[3,1,4]{2,1,0:T(1,128)} %bitcast.24, s32[1,4]{1,0:T(1,128)} %owner_hbm.1, f32[16,32,128]{2,1,0:T(8,128)} %c_src_hbm.1, f32[16,32,128]{2,1,0:T(8,128)} %c_shift_hbm.1, f32[16,32,128]{2,1,0:T(8,128)} %c_start_hbm.1, ...), custom_call_target="tpu_custom_call" | custom-call | tf_op jit(solution)/shard_map/pallas_call | solution.py:719
  42.1 1.4 %shard_map.104 = (f32[16,32,128]{2,1,0:T(8,128)}, f32[1024,128]{1,0:T(8,128)}, f32[2]{0:T(128)}) custom-call(f32[8,128]{1,0:T(8,128)S(1)} %get-tuple-element.9.norms, f32[16,32,128]{2,1,0:T(8,128)S(1)} %get-tuple-element.10.pot, f32[1024,128]{1,0:T(8,128)S(1)} %get-tuple-element.11.rows), custom_call_target="tpu_custom_call" | custom-call | tf_op jit(solution)/shard_map/pallas_call | solution.py:768

commit v4 on v3

--- a/solution.py
+++ b/solution.py
@@ -1,6 +1,5 @@
 import functools
 import itertools
-import math
 
 import jax
 import jax.numpy as jnp
@@ -23,7 +22,6 @@
 CH = 16
 PIECES = 2
 FCH = 16
-DIRS = [d for d in itertools.product((-1, 0, 1), repeat=3) if any(d)]
 FPLANE = SIDE + 8
 
 
@@ -33,6 +31,11 @@
 
 def iota(shape, dim):
     return lax.broadcasted_iota(jnp.int32, shape, dim)
+
+
+def directions(sizes):
+    z_steps = (0, 1) if sizes[2] == 2 else (-1, 0, 1)
+    return [d for d in itertools.product((-1, 0, 1), (-1, 0, 1), z_steps) if any(d)]
 
 
 def turn(x, by):
@@ -60,7 +63,6 @@
     f_src,
     f_shift,
     f_start,
-    in_sem,
     H0,
     P1,
     W1,
@@ -110,6 +112,8 @@
     inside = pl.ds(DEEP, nx)
     gx, gy, gz = lax.axis_index("gx"), lax.axis_index("gy"), lax.axis_index("gz")
     me = gy * n_gz + gz
+    DIRS = directions(sizes)
+    pair = sizes[2] == 2
     V = (V0, V1)
     P0, W0, E0 = (H0.at[f] for f in range(3))
     zero_rows = jnp.zeros((rows, LANES), jnp.float32)
@@ -119,7 +123,7 @@
         return (gx, rank // n_gz, rank % n_gz)
 
     loads = [
-        pltpu.make_async_copy(source, target, in_sem.at[i])
+        pltpu.make_async_copy(source, target, h_send.at[i])
         for i, (source, target) in enumerate(
             (
                 (c_start_hbm, H0.at[0, inside, inner]),
@@ -247,32 +251,38 @@
                     v[pl.ds(start_of(2 * X + e) - 1, 1)] = low
                     v[pl.ds(start_of(2 * X + e) + SIDE, 1)] = top
 
-    def beside_fine(v, par, x, r):
+    def beside_fine(cells, v, par, x, r):
+        def cell(x):
+            if (x, r) not in cells:
+                cells[x, r] = v[pl.ds(start_of(x) + r, FCH)]
+            return cells[x, r]
+
         at = start_of(x) + r
-        u = v[pl.ds(at, FCH)]
+        u = cell(x)
         ghost = G[par, x // 2, pl.ds(r, FCH)]
         zu = jnp.where(z_pos < SIDE - 1, turn(u, -1), ghost)
         zl = jnp.where(z_pos > 0, turn(u, 1), ghost)
-        across = v[pl.ds(at + FPLANE, FCH)] + v[pl.ds(at - FPLANE, FCH)]
         along = v[pl.ds(at + 1, FCH)] + v[pl.ds(at - 1, FCH)]
-        return u, (across + along) + (zu + zl)
+        return u, ((cell(x + 1) + cell(x - 1)) + along) + (zu + zl)
 
     def fine_sweep(vp, par):
-        for x in range(SIDE):
-            for r in range(0, SIDE, FCH):
-                at = pl.ds(r, FCH)
-                u, s = beside_fine(V[vp], par, x, r)
+        cells = {}
+        for r in range(0, SIDE, FCH):
+            at = pl.ds(r, FCH)
+            for x in range(SIDE):
+                u, s = beside_fine(cells, V[vp], par, x, r)
                 V[1 - vp][pl.ds(start_of(x) + r, FCH)] = KEEP * u + FW[x, at] * (FS[x, at] + s)
 
     def fine_remainder(vp, par):
+        cells = {}
         total = jnp.zeros(wide, jnp.float32)
-        for X in range(FOOT):
-            for r in range(0, SIDE, FCH):
-                at = pl.ds(r, FCH)
+        for r in range(0, SIDE, FCH):
+            at = pl.ds(r, FCH)
+            for X in range(FOOT):
                 t = None
                 for e in range(2):
                     x = 2 * X + e
-                    u, s = beside_fine(V[vp], par, x, r)
+                    u, s = beside_fine(cells, V[vp], par, x, r)
                     w = (FS[x, at] - FD[x, at] * u) + s
                     total = total + w * w
                     t = w if t is None else t + w
@@ -291,9 +301,9 @@
                 for h in range(2):
                     even = T[X, pl.ds(16 * h, 8, stride=2), :]
                     odd = T[X, pl.ds(16 * h + 1, 8, stride=2), :]
-                    both = even + odd
-                    halves.append(both + turn(both, -1))
-                packed.append(jnp.where(lane % 2 == 0, halves[0], turn(halves[1], 1)) * 0.125)
+                    pairs = even + odd
+                    halves.append(pairs + turn(pairs, 1 if h else -1))
+                packed.append(jnp.where(lane % 2 == 0, halves[0], halves[1]) * 0.125)
             for j in range(slots):
                 acc = turn(packed[0], -SIDE * j)
                 for k in range(1, 4):
@@ -365,63 +375,84 @@
             acc = jnp.where(tall // (2 * DEEP) == x, turn(F[DEEP + x, inner], 2 * DEEP * x + DEEP), acc)
         pk[f] = acc
 
-    def regions(fields, depth, d):
+    def sent_from(fields, depth, d):
         dx, dy, dz = d
-        x_src = {0: inside, -1: pl.ds(DEEP, depth), 1: pl.ds(DEEP + nx - depth, depth)}[dx]
-        x_dst = {0: inside, -1: pl.ds(DEEP + nx, depth), 1: pl.ds(DEEP - depth, depth)}[dx]
         if dz == 0:
+            x_src = {0: inside, -1: pl.ds(DEEP, depth), 1: pl.ds(DEEP + nx - depth, depth)}[dx]
             y_src = {0: inner, -1: pl.ds(first, 8), 1: pl.ds(first + ny - 8, 8)}[dy]
-            y_dst = {0: inner, -1: pl.ds(first + ny, 8), 1: pl.ds(PAD, 8)}[dy]
-            return H0.at[fields, x_src, y_src], H0.at[fields, x_dst, y_dst]
-        y_src = {0: pl.ds(0, ny), -1: pl.ds(0, 8), 1: pl.ds(ny - 8, 8)}[dy]
-        y_dst = {0: pl.ds(8, ny), -1: pl.ds(8 + ny, 8), 1: pl.ds(0, 8)}[dy]
-        return pk.at[fields, y_src], zs.at[fields, {0: 0, -1: 1, 1: 2}[dx], 0 if dz < 0 else 1, y_dst]
+            return H0.at[fields, x_src, y_src]
+        return pk.at[fields, {0: pl.ds(0, ny), -1: pl.ds(0, 8), 1: pl.ds(ny - 8, 8)}[dy]]
+
+    def lands_at(fields, depth, d, z_side):
+        dx, dy, dz = d
+        if dz == 0:
+            x_dst = {0: inside, 1: pl.ds(DEEP + nx, depth), -1: pl.ds(DEEP - depth, depth)}[dx]
+            y_dst = {0: inner, 1: pl.ds(first + ny, 8), -1: pl.ds(PAD, 8)}[dy]
+            return H0.at[fields, x_dst, y_dst]
+        y_dst = {0: pl.ds(8, ny), 1: pl.ds(8 + ny, 8), -1: pl.ds(0, 8)}[dy]
+        return zs.at[fields, {0: 0, 1: 1, -1: 2}[dx], z_side, y_dst]
+
+    def back(d):
+        return (-d[0], -d[1], d[2] if pair else -d[2])
+
+    def device(d):
+        return (gx + d[0], gy + d[1], (1 - gz if d[2] else gz) if pair else gz + d[2])
+
+    def own_side(d):
+        return gz if pair else (0 if d[2] > 0 else 1)
+
+    def their_side(d):
+        return 1 - gz if pair else (0 if d[2] < 0 else 1)
 
     def there(d):
         tests = []
-        for step, at, count in zip(d, (gx, gy, gz), sizes):
+        for step, at, count in zip(d[:2] if pair else d, (gx, gy, gz), sizes):
             if step < 0:
                 tests.append(at > 0)
             if step > 0:
                 tests.append(at < count - 1)
-        return functools.reduce(jnp.logical_and, tests)
-
-    def flag(d):
-        return tuple(abs(v) if n == 2 else v for v, n in zip(d, sizes))
-
-    flags = sorted({flag(d) for d in DIRS})
+        return functools.reduce(jnp.logical_and, tests) if tests else None
+
+    def when_there(d):
+        test = there(d)
+        return (lambda f: f()) if test is None else pl.when(test)
 
     def halo_copy(kind, fields, depth, i):
         d = DIRS[i]
-        source, target = regions(fields, depth, d)
         return pltpu.make_async_remote_copy(
-            src_ref=source,
-            dst_ref=target,
-            send_sem=h_send.at[flags.index(flag(d))],
-            recv_sem=h_recv.at[kind, flags.index(flag(tuple(-v for v in d)))],
-            device_id=(gx + d[0], gy + d[1], gz + d[2]),
+            src_ref=sent_from(fields, depth, d),
+            dst_ref=lands_at(fields, depth, back(d), their_side(d)),
+            send_sem=h_send.at[i],
+            recv_sem=h_recv.at[kind, DIRS.index(back(d))],
+            device_id=device(d),
             device_id_type=MESH,
         )
 
     def halo_wait(kind, fields, depth, i):
         d = DIRS[i]
-        _, target = regions(fields, depth, tuple(-v for v in d))
+        target = lands_at(fields, depth, d, own_side(d))
         return pltpu.make_async_remote_copy(
             src_ref=target,
             dst_ref=target,
-            send_sem=h_send.at[flags.index(flag(d))],
-            recv_sem=h_recv.at[kind, flags.index(flag(d))],
-            device_id=(gx + d[0], gy + d[1], gz + d[2]),
+            send_sem=h_send.at[i],
+            recv_sem=h_recv.at[kind, i],
+            device_id=device(d),
             device_id_type=MESH,
         )
 
     def clear_halos():
         for d in DIRS:
-
-            @pl.when(jnp.logical_not(there(d)))
-            def _():
-                _, target = regions(pl.ds(0, 3), DEEP, tuple(-v for v in d))
-                target[...] = jnp.zeros(target.shape, jnp.float32)
+            if there(d) is not None:
+
+                @pl.when(jnp.logical_not(there(d)))
+                def _():
+                    target = lands_at(pl.ds(0, 3), DEEP, d, own_side(d))
+                    target[...] = jnp.zeros(target.shape, jnp.float32)
+
+        if pair:
+            for f in range(3):
+                for a in range(3):
+                    zs[f, a, 1 - gz] = zero_rows
 
     far_first = sorted(range(len(DIRS)), key=lambda i: -sum(map(abs, DIRS[i])))
     flat = [i for i in far_first if DIRS[i][2] == 0]
@@ -431,12 +462,12 @@
 
     def send_halo(kind, fields, depth, which):
         for i in which:
-            pl.when(there(DIRS[i]))(halo_copy(kind, fields, depth, i).start)
+            when_there(DIRS[i])(halo_copy(kind, fields, depth, i).start)
 
     def wait_halo(kind, fields, depth):
         for i in reversed(far_first):
 
-            @pl.when(there(DIRS[i]))
+            @when_there(DIRS[i])
             def _():
                 halo_copy(kind, fields, depth, i).wait_send()
                 halo_wait(kind, fields, depth, i).wait_recv()
@@ -461,9 +492,9 @@
             F1[X, block] = value
 
     def reach(depth):
-        for X in range(DEEP - depth, DEEP + nx + depth):
-            left = depth - max(DEEP - X, X - (DEEP + nx - 1), 0)
-            for r in range(PAD, PAD + rows, 8):
+        for r in range(PAD, PAD + rows, 8):
+            for X in range(DEEP - depth, DEEP + nx + depth):
+                left = depth - max(DEEP - X, X - (DEEP + nx - 1), 0)
                 rest = left - (0 if first <= r < first + ny else 1)
                 if rest >= 0:
                     yield X, r, 2 if rest else 1
@@ -471,17 +502,27 @@
     lane0, lane127 = lane == 0, lane == LANES - 1
 
     def sweep(source, target, comp, depth, squares=False):
-        U0, U1 = source
         total = zero_tile
+        cells = {}
+
+        def cell(t, X, r):
+            if (t, X, r) not in cells:
+                cells[t, X, r] = source[t][X, pl.ds(r, 8)]
+            return cells[t, X, r]
+
         for X, r, tiles in reach(depth):
             here, up, down = pl.ds(r, 8), pl.ds(r + 1, 8), pl.ds(r - 1, 8)
-            u = (U0[X, here], U1[X, here])
-            prev = [turn(v, 1) for v in u]
-            nxt = [turn(v, -1) for v in u]
+            u = (cell(0, X, r), cell(1, X, r))
+            if tiles == 2:
+                prev = [turn(v, 1) for v in u]
+                nxt = [turn(v, -1) for v in u]
             for t in range(tiles):
                 U = source[t]
-                z = jnp.where(lane0, prev[1 - t], prev[t]) + jnp.where(lane127, nxt[1 - t], nxt[t])
-                s = ((U[X - 1, here] + U[X + 1, here]) + (U[X, up] + U[X, down])) + z
+                if tiles == 2:
+                    z = jnp.where(lane0, prev[1 - t], prev[t]) + jnp.where(lane127, nxt[1 - t], nxt[t])
+                else:
+                    z = turn(jnp.where(lane127, u[1], u[0]), 1) + turn(jnp.where(lane0, u[1], u[0]), -1)
+                s = ((cell(t, X - 1, r) + cell(t, X + 1, r)) + (U[X, up] + U[X, down])) + z
                 if comp is not None:
                     s = s + comp[t][X, here]
                 target[t][X, here] = KEEP * u[t] + (W0, W1)[t][X, here] * s
@@ -706,7 +747,7 @@
     f32 = jnp.float32
     devices = n_gx * group
     direct = devices <= 64
-    flags = math.prod(2 if n == 2 else 3 for n in sizes) - 1
+    flags = len(directions(sizes))
     assert 2 * DEEP * nx == LANES == nz and slots * SIDE == LANES and nx == FOOT
     vmem = pl.BlockSpec(memory_space=pltpu.VMEM)
     smem = pl.BlockSpec(memory_space=pltpu.SMEM)
@@ -729,7 +770,6 @@
             rows,
             rows,
             rows,
-            dma((8,)),
         ]
         + [pltpu.VMEM((3,) + ring.shape, f32)]
         + [ring] * 7

time: 43.7 us -> 43 us (0.984)
  Pallas kernels: 42.9 us -> 42.2 us
    pallas_call x1, Pallas kernels: 41.5 us -> 40.7 us  [local(): pl.pallas_call(functools.partial(kernel, sizes), out_shape=(pltpu.VMEM((n...]
where the time goes in v4:
time: 43 us; the launch traced here: 42.8 us
  Pallas kernels  42.2 us (98%)
  between operations  0.64 us (1%)
    pallas_call x1, Pallas kernels, local(): pl.pallas_call(functools.partial(kernel, sizes), out_shape=(pltpu.VMEM((n...  40.7 us
    pallas_call x1, Pallas kernels, local(): pl.pallas_call(finish, out_shape=(jax.ShapeDtypeStruct(pot.shape, f32), j...  1.43 us

profile of v4, /device:TPU:0, one launch (start us, length us, event | category | flops | bytes accessed | tf_op | source)
XLA Modules:
  0.0 42.8 jit_solution(11963047726081216670)
XLA Ops:
  0.6 40.7 %shard_map.103 = (f32[16,32,128]{2,1,0:T(8,128)S(1)}, f32[1024,128]{1,0:T(8,128)S(1)}, f32[8,128]{1,0:T(8,128)S(1)}) custom-call(s32[3,1,4]{2,1,0:T(1,128)} %bitcast.24, s32[1,4]{1,0:T(1,128)} %owner_hbm.1, f32[16,32,128]{2,1,0:T(8,128)} %c_src_hbm.1, f32[16,32,128]{2,1,0:T(8,128)} %c_shift_hbm.1, f32[16,32,128]{2,1,0:T(8,128)} %c_start_hbm.1, ...), custom_call_target="tpu_custom_call" | custom-call | tf_op jit(solution)/shard_map/pallas_call | solution.py:760
  41.4 1.4 %shard_map.104 = (f32[16,32,128]{2,1,0:T(8,128)}, f32[1024,128]{1,0:T(8,128)}, f32[2]{0:T(128)}) custom-call(f32[8,128]{1,0:T(8,128)S(1)} %get-tuple-element.9.norms, f32[16,32,128]{2,1,0:T(8,128)S(1)} %get-tuple-element.10.pot, f32[1024,128]{1,0:T(8,128)S(1)} %get-tuple-element.11.rows), custom_call_target="tpu_custom_call" | custom-call | tf_op jit(solution)/shard_map/pallas_call | solution.py:808
